TPU v7x, 32 devices: a whole 2x2x4 slice. The times are simulated.
32 devices in a mesh: il: 2 (over core), xl: 4 (over y, x), ta: 4 (over z).
Axes of the slice: x: 2, y: 2, z: 4, core: 2. Of those that a mesh axis runs over, the one named last changes fastest.
Arguments:
- traces: float32 [32, 832, 1024], P('il', 'xl', 'ta'), may hold values from -6 to 6
- bin_steps: int32 [2, 32, 832], P(None, 'il', 'xl'), may hold values from -1 to 1
Outputs:
- regridded: float32 [16, 416, 1536], P('il', 'xl', 'ta')
Inputs may be any that keep to these rules, and one draw needn't show every extreme that they name: `bin_steps`: every entry is -1, 0 or 1.
All inputs are finite; a program needn't handle non-finite values.
Results may differ from a plain program's by a relative error of at most 0.0001.
Values sent between devices are 32-bit elements; how exact they have to be, the bound alone decides.
A program may use at most 128 MiB of HBM per device.

v0:
```python
import functools

import numpy as np
import jax
import jax.numpy as jnp
from jax import lax
from jax.experimental import pallas as pl
from jax.experimental.pallas import tpu as pltpu
from jax.sharding import PartitionSpec as P

TAPS = 16
P_SIZE = 3
Q = 2
AHEAD = 2
MESH = pl.DeviceIdType.MESH
F32, BF16 = jnp.float32, jnp.bfloat16


def lanczos_table(span):
    reach = TAPS // 2
    rows = np.arange(span + 2 * reach)[:, None] - reach
    cols = np.arange(span * P_SIZE // Q)[None, :]
    offset = (cols * Q - rows * P_SIZE).astype(np.float64) / P_SIZE
    weights = np.sinc(offset) * np.sinc(offset / reach)
    return np.where(np.abs(offset) < reach, weights, 0.0).astype(np.float32)


def split_table(table):
    high = table.astype(BF16)
    low = (table - high.astype(np.float32)).astype(BF16)
    return high, low


def halves(values):
    high = values.astype(BF16)
    low = (values - high.astype(F32)).astype(BF16)
    return high, low


def dot(a, b):
    return jnp.dot(a, b, preferred_element_type=F32)


def column_ranges(n_cols):
    split = n_cols // 2 // 16 * 16
    if split < 16 or n_cols % 16:
        raise ValueError("column count")
    ranges = []
    for start, stop in ((0, split), (split, n_cols)):
        first = start // 2 // 8 * 8
        last = (stop - 1) // 2 + 2
        ranges.append((start, stop, first, (last + 1 - first + 7) // 8 * 8))
    return ranges


def binning(n_xl, n_ta, traces, steps_hbm, t_high_hbm, t_low_hbm, main, halo_out, x, edge_x, steps, t_high, t_low, keys,
            acc, acc_ends, one_hot_low, one_hot_high, rim_send, rim_recv, il_recv, il_recv_ends, corner_recv, halo_send, halo_recv, load_sem, edge_sem, table_sem,
            send_sem, recv_sem):
    n_rows, n_cols, span = x.shape
    n_pairs = n_rows // 2
    own_cols = n_cols // 2
    reach = TAPS // 2
    il, xl, ta = lax.axis_index("il"), lax.axis_index("xl"), lax.axis_index("ta")
    other = 1 - il
    has_xl = (xl < n_xl - 1, xl > 0)
    has_ta = (ta < n_ta - 1, ta > 0)
    xl_at, ta_at = (xl + 1, xl - 1), (ta + 1, ta - 1)

    def when(condition, work):
        pl.when(condition)(work)

    def pair(p):
        return jnp.where(il == 0, n_pairs - 1 - p, p)

    step_load = pltpu.make_async_copy(steps_hbm, steps, table_sem.at[2])
    step_load.start()
    edge_loads = [pltpu.make_async_copy(traces.at[:, pl.ds(start, 8)], edge_x.at[d], edge_sem.at[d])
                  for d, start in enumerate((n_cols - 8, 0))]
    for load in edge_loads:
        load.start()
    loads = []
    for p in range(n_pairs):
        rows = pl.ds(2 * pair(p), 2)
        loads.append(pltpu.make_async_copy(traces.at[rows], x.at[rows], load_sem.at[p]))

    barrier = pltpu.get_barrier_semaphore()

    def greet(partner):
        pl.semaphore_signal(barrier, inc=1, device_id=partner, device_id_type=MESH)

    greet({"il": other})
    for d in range(2):
        def both(d=d):
            greet({"xl": xl_at[d]})
            greet({"il": other, "xl": xl_at[d]})
        when(has_xl[d], both)
        when(has_ta[d], lambda d=d: greet({"ta": ta_at[d]}))

    def load_pair(p):
        rows = pl.ds(2 * pair(p), 2)
        pltpu.make_async_copy(traces.at[rows], x.at[rows], load_sem.at[p]).start()

    pl.loop(0, n_pairs)(load_pair)
    table_loads = [pltpu.make_async_copy(t_high_hbm, t_high, table_sem.at[0]),
                   pltpu.make_async_copy(t_low_hbm, t_low, table_sem.at[1])]
    for load in table_loads:
        load.start()

    acc[...] = jnp.zeros_like(acc)
    acc_ends[...] = jnp.zeros_like(acc_ends)
    one_hots = (one_hot_low, one_hot_high)
    step_load.wait()
    ranges = column_ranges(n_cols)
    col = lax.broadcasted_iota(jnp.int32, (n_rows, n_cols), 1)
    bin_col = lax.shift_right_logical(col, 1) + steps[1] + 1
    bin_row = steps[0] + 1
    for k, (start, stop, first, height) in enumerate(ranges):
        code = bin_row * height + bin_col - first
        for p in range(n_pairs):
            keys[k, p, :, :2 * (stop - start)] = jnp.concatenate(
                [code[2 * p: 2 * p + 1, start:stop], code[2 * p + 1: 2 * p + 2, start:stop]], axis=1)

    def one_hot(key, height):
        rows = lax.broadcasted_iota(jnp.int32, (height, key.shape[1]), 0)
        return jnp.where(rows == key, 1.0, 0.0).astype(BF16)

    def totals(chosen, values):
        high, low = halves(values)
        return (dot(chosen, high) + dot(chosen, low), dot(chosen, jnp.ones((values.shape[0], 128), BF16)))

    lane = lax.broadcasted_iota(jnp.int32, (1, 128), 1)
    is_first, is_last = lane < reach, lane >= 128 - reach

    def pair_values(at, start, stop, samples):
        return jnp.concatenate([x[2 * at, start:stop, samples], x[2 * at + 1, start:stop, samples]], axis=0)

    def bin_edges(p):
        at = pair(p)
        loads[p].wait()
        for k, (start, stop, first, height) in enumerate(ranges):
            chosen = one_hot(keys[k, at][:, :2 * (stop - start)], 3 * height)
            one_hots[k][at] = chosen
            values = jnp.where(lane < 64, pair_values(at, start, stop, slice(0, 128)),
                               pair_values(at, start, stop, slice(span - 128, span)))
            high = values.astype(BF16)
            low = jnp.where(is_first | is_last, values - high.astype(F32), 1.0).astype(BF16)
            sums = dot(chosen, jnp.concatenate([high, low], axis=1))
            ends = jnp.where(is_first | is_last, sums[:, :128], 0.0) + sums[:, 128:]
            for r in range(3):
                acc_ends[at + r, first: first + height, :] += ends[r * height: (r + 1) * height]

    def bin_pair(p):
        at = pair(p)
        for k, (start, stop, first, height) in enumerate(ranges):
            chosen = one_hots[k][at]
            high, low = halves(pair_values(at, start, stop, slice(0, span)))
            sums = dot(chosen, high) + dot(chosen, low)
            for r in range(3):
                acc[at + r, first: first + height, :] += sums[r * height: (r + 1) * height]

    def remote(src, dst, slot, partner):
        return pltpu.make_async_remote_copy(src_ref=src, dst_ref=dst, send_sem=send_sem.at[slot],
                                            recv_sem=recv_sem.at[slot], device_id=partner, device_id_type=MESH)

    rim_row = jnp.where(il == 0, n_pairs + 1, 0)
    own_row = jnp.where(il == 0, n_pairs, 1)
    to_other = remote(acc.at[rim_row], il_recv, 0, {"il": other})
    ends_to_other = remote(acc_ends.at[rim_row], il_recv_ends, 7, {"il": other})
    rims = [(remote(rim_send.at[d], rim_recv.at[d], 1 + d, {"xl": xl_at[d]}),
             remote(rim_send.at[d, rim_row], corner_recv.at[d], 3 + d, {"il": other, "xl": xl_at[d]}))
            for d in range(2)]

    row = lax.broadcasted_iota(jnp.int32, (n_rows, n_cols), 0)
    rim_bin = bin_row + lax.shift_right_logical(row, 1)
    for load in edge_loads:
        load.wait()
    for d, (start, column) in enumerate(((n_cols - 8, own_cols + 1), (0, 0))):
        target = jnp.where(bin_col == column, rim_bin, -1)
        key = jnp.concatenate([target[i: i + 1, start: start + 8] for i in range(n_rows)], axis=1)
        sums, folds = totals(one_hot(key, (n_pairs + 2 + 7) // 8 * 8), edge_x[d].reshape(n_rows * 8, span))
        for r in range(n_pairs + 2):
            rim_send[d, r, :, :span] = sums[r: r + 1]
            rim_send[d, r, :, span:] = jnp.where(is_first, sums[r: r + 1, :128], jnp.where(
                is_last, sums[r: r + 1, span - 128:], folds[r: r + 1]))
    peers = 1
    for d in range(2):
        peers = peers + jnp.where(has_xl[d], 2, 0) + jnp.where(has_ta[d], 1, 0)
    pl.semaphore_wait(barrier, peers)
    for d in range(2):
        def go(d=d):
            for copy in rims[d]:
                copy.start()
        when(has_xl[d], go)
    bin_edges(0)
    ends_to_other.start()
    for p in range(1, n_pairs):
        bin_edges(p)
    for p in range(AHEAD):
        bin_pair(p)
        if p == 0:
            to_other.start()
    ends_to_other.wait_recv()
    acc_ends[own_row] = acc_ends[own_row] + il_recv_ends[...]
    for d, column in enumerate((1, own_cols)):
        def add_ends(d=d, column=column):
            for copy in rims[d]:
                copy.wait_recv()
            for r in range(1, n_pairs + 1):
                acc_ends[r, column: column + 1, :] += rim_recv[d, r, :, span:]
            acc_ends[own_row, column: column + 1, :] += corner_recv[d, :, span:]
        when(has_xl[1 - d], add_ends)

    halos = [remote(halo_send.at[d], halo_recv.at[d], 5 + d, {"ta": ta_at[d]}) for d in range(2)]
    for b in range(n_pairs):
        lanes = slice(b * 128, b * 128 + own_cols)
        ends = acc_ends[b + 1, 1: own_cols + 1, :].T
        factor = 1.0 / jnp.maximum(ends[64:64 + reach], 1.0)
        halo_send[0, :, lanes] = ends[128 - reach:] * factor
        halo_send[1, :, lanes] = ends[:reach] * factor
    for d in range(2):
        when(has_ta[d], halos[d].start)

    for p in range(AHEAD, n_pairs):
        bin_pair(p)
        if p == 0:
            to_other.start()
    to_other.wait_recv()
    acc[own_row] = acc[own_row] + il_recv[...]
    for d, column in enumerate((1, own_cols)):
        def add(d=d, column=column):
            for r in range(1, n_pairs + 1):
                acc[r, column: column + 1, :] += rim_recv[d, r, :, :span]
            acc[own_row, column: column + 1, :] += corner_recv[d, :, :span]
        when(has_xl[1 - d], add)
    for load in table_loads:
        load.wait()
    for b in range(n_pairs):
        fold = jnp.broadcast_to(acc_ends[b + 1, 1: own_cols + 1, 64:65], (own_cols, 128))
        factor = 1.0 / jnp.maximum(fold, 1.0)
        sums = acc[b + 1, 1: own_cols + 1, :]
        high, low = halves(sums * jnp.concatenate([factor] * (span // 128), axis=1))
        main[b] = dot(high, t_high[...]) + (dot(low, t_high[...]) + dot(high, t_low[...]))
    for d in range(2):
        def arrived(d=d):
            halos[d].wait_recv()
            halo_out[d] = halo_recv[d]

        def absent(d=d):
            halo_out[d] = jnp.zeros_like(halo_recv[d])
        when(has_ta[1 - d], arrived)
        when(jnp.logical_not(has_ta[1 - d]), absent)
    for d in range(2):
        when(has_ta[d], halos[d].wait_send)
        def sent(d=d):
            for copy in rims[d]:
                copy.wait_send()
        when(has_xl[d], sent)
    to_other.wait_send()
    ends_to_other.wait_send()


def finish(main, halo, t_edge, out, staged, out_sem):
    n_pairs, own_cols, width = main.shape
    inner = pl.ds(128, width - 256)
    writes = [pltpu.make_async_copy(main.at[:, :, inner], out.at[:, :, inner], out_sem.at[n_pairs, 0])]
    writes[0].start()
    for b in range(n_pairs):
        lanes = slice(b * 128, (b + 1) * 128)
        edges = jnp.concatenate([halo[0, :, lanes], halo[1, :, lanes]], axis=0)
        high = edges.astype(BF16).astype(F32)
        terms = jnp.concatenate([high, edges - high, high], axis=0).T[:own_cols].astype(BF16)
        ends = dot(terms, t_edge[...])
        for d, start in enumerate((0, width - 128)):
            staged[b, d] = main[b, :, start: start + 128] + ends[:, d * 128: (d + 1) * 128]
            write = pltpu.make_async_copy(staged.at[b, d], out.at[b, :, pl.ds(start, 128)], out_sem.at[b, d])
            write.start()
            writes.append(write)
    for write in writes:
        write.wait()


def shards(n_xl, n_ta, traces, bin_steps):
    n_rows, n_cols, span = traces.shape
    n_pairs, own_cols = n_rows // 2, n_cols // 2
    reach = TAPS // 2
    padded = (own_cols + 2 + 7) // 8 * 8
    width = span + 128
    out_span = span * P_SIZE // Q
    table = lanczos_table(span)
    t_high, t_low = split_table(table[reach:-reach])
    edge_high, edge_low = split_table(np.concatenate([table[:reach], table[-reach:]]))
    t_edge = np.concatenate([edge_high, edge_high, edge_low])
    t_edge = np.concatenate([t_edge[:, :128], t_edge[:, -128:]], axis=1)
    if out_span < 384:
        raise ValueError("sample count")
    vmem = pl.BlockSpec(memory_space=pltpu.VMEM)
    hbm = pl.BlockSpec(memory_space=pltpu.HBM)
    main, halo = pl.pallas_call(
        functools.partial(binning, n_xl, n_ta),
        out_shape=(pltpu.VMEM((n_pairs, own_cols, out_span), F32), pltpu.VMEM((2, reach, n_pairs * 128), F32)),
        in_specs=[hbm] * 4,
        out_specs=[vmem] * 2,
        scratch_shapes=[
            pltpu.VMEM((n_rows, n_cols, span), F32),
            pltpu.VMEM((2, n_rows, 8, span), F32),
            pltpu.VMEM((2, n_rows, n_cols), jnp.int32),
            pltpu.VMEM(t_high.shape, BF16),
            pltpu.VMEM(t_low.shape, BF16),
            pltpu.VMEM((2, n_pairs, 1, (n_cols + 32 + 127) // 128 * 128), jnp.int32),
            pltpu.VMEM((n_pairs + 2, padded, span), F32),
            pltpu.VMEM((n_pairs + 2, padded, 128), F32),
            *[pltpu.VMEM((n_pairs, 3 * height, 2 * (stop - start)), BF16)
              for start, stop, _, height in column_ranges(n_cols)],
            pltpu.VMEM((2, n_pairs + 2, 1, width), F32),
            pltpu.VMEM((2, n_pairs + 2, 1, width), F32),
            pltpu.VMEM((padded, span), F32),
            pltpu.VMEM((padded, 128), F32),
            pltpu.VMEM((2, 1, width), F32),
            pltpu.VMEM((2, reach, n_pairs * 128), F32),
            pltpu.VMEM((2, reach, n_pairs * 128), F32),
            pltpu.SemaphoreType.DMA((n_pairs,)),
            pltpu.SemaphoreType.DMA((2,)),
            pltpu.SemaphoreType.DMA((3,)),
            pltpu.SemaphoreType.DMA((8,)),
            pltpu.SemaphoreType.DMA((8,)),
        ],
        compiler_params=pltpu.CompilerParams(collective_id=0, has_side_effects=True, vmem_limit_bytes=24 * 2**20),
        name="binning",
    )(*[pltpu.with_memory_space_constraint(a, pltpu.HBM) for a in (traces, bin_steps, jnp.asarray(t_high), jnp.asarray(t_low))])
    return pl.pallas_call(
        finish,
        out_shape=jax.ShapeDtypeStruct((n_pairs, own_cols, out_span), F32),
        in_specs=[vmem] * 3,
        out_specs=hbm,
        scratch_shapes=[pltpu.VMEM((n_pairs, 2, own_cols, 128), F32), pltpu.SemaphoreType.DMA((n_pairs + 1, 2))],
        compiler_params=pltpu.CompilerParams(vmem_limit_bytes=16 * 2**20),
        name="finish",
    )(main, halo, jnp.asarray(t_edge))


def solution(mesh):
    if mesh.shape["il"] != 2:
        raise ValueError("il size")
    return jax.shard_map(
        functools.partial(shards, mesh.shape["xl"], mesh.shape["ta"]),
        mesh=mesh,
        in_specs=(P("il", "xl", "ta"), P(None, "il", "xl")),
        out_specs=P("il", "xl", "ta"),
        check_vma=False,
    )
```

profile of v0, /device:TPU:0, one launch (start us, length us, event | category | flops | bytes accessed | tf_op | source)
XLA Modules:
  0.0 11.7 jit_solution(2873683139957117509)
XLA Ops:
  0.0 0.0 copy-start
  0.0 10.4 %binning.1 = (f32[8,104,384]{2,1,0:T(8,128)S(1)}, f32[2,8,1024]{2,1,0:T(8,128)S(1)}) custom-call(f32[16,208,256]{2,1,0:T(8,128)} %traces.1, s32[2,16,208]{2,1,0:T(8,128)} %steps_hbm.1, bf16[256,384]{1,0:T(8,128)(2,1)} %constant.6.clone.t_high_hbm, bf16[256,384]{1,0:T(8,128)(2,1)} %constant.7.clone.t_low_hbm), custom_call_target="tpu_custom_call" | custom-call | tf_op jit(solution)/shard_map/binning/pallas_call | solution.py:298
  10.4 0.0 copy-done
  10.4 1.3 %finish.1 = f32[8,104,384]{2,1,0:T(8,128)} custom-call(f32[8,104,384]{2,1,0:T(8,128)S(1)} %get-tuple-element.7.main, f32[2,8,1024]{2,1,0:T(8,128)S(1)} %get-tuple-element.8.halo, bf16[48,256]{1,0:T(8,128)(2,1)S(1)} %copy-done), custom_call_target="tpu_custom_call" | custom-call | tf_op jit(solution)/shard_map/finish/pallas_call | solution.py:330
Async XLA Ops:
  0.0 10.4 %copy-start = (bf16[48,256]{1,0:T(8,128)(2,1)S(1)}, bf16[48,256]{1,0:T(8,128)(2,1)}, u32[]{:S(2)}) copy-start(bf16[48,256]{1,0:T(8,128)(2,1)} %constant.8.clone.t_edge) | copy-start | bytes 73732
where the time goes:
time: 11.9 us; the launch traced here: 11.7 us
  Pallas kernels  11.7 us (98%)
    pallas_call x1, Pallas kernels, shards(): pl.pallas_call(functools.partial(binning, n_xl, n_ta), out_shape=(pltpu.V...  10.4 us
    pallas_call x1, Pallas kernels, shards(): pl.pallas_call(finish, out_shape=jax.ShapeDtypeStruct((n_pairs, own_cols,...  1.28 us

commit v1 on v0

v1 whole, which is shorter than its diff:
```python
import functools

import numpy as np
import jax
import jax.numpy as jnp
from jax import lax
from jax.experimental import pallas as pl
from jax.experimental.pallas import tpu as pltpu
from jax.sharding import PartitionSpec as P

TAPS = 16
P_SIZE = 3
Q = 2
REACH = TAPS // 2
LANES = 128
MESH = pl.DeviceIdType.MESH
F32, BF16 = jnp.float32, jnp.bfloat16


def lanczos_table(span):
    rows = np.arange(span + 2 * REACH)[:, None] - REACH
    cols = np.arange(span * P_SIZE // Q)[None, :]
    offset = (cols * Q - rows * P_SIZE).astype(np.float64) / P_SIZE
    weights = np.sinc(offset) * np.sinc(offset / REACH)
    return np.where(np.abs(offset) < REACH, weights, 0.0).astype(np.float32)


def split_table(table):
    high = table.astype(BF16)
    low = (table - high.astype(np.float32)).astype(BF16)
    return high, low


def halves(values):
    high = values.astype(BF16)
    low = (values - high.astype(F32)).astype(BF16)
    return high, low


def dot(a, b):
    return jnp.dot(a, b, preferred_element_type=F32)


def column_ranges(n_cols):
    own_cols, rest = n_cols // 2, n_cols - LANES
    if own_cols % 8 or rest % 16 or not LANES < 2 * rest <= 2 * LANES:
        raise ValueError("column count")
    height = (LANES // 2 + 1 + 7) // 8 * 8
    first = (LANES // 2 - 1) // 8 * 8
    return (0, LANES, 0, height), (LANES, n_cols, first, own_cols - first)


def binning(n_xl, n_ta, traces, steps_hbm, t_high_hbm, t_low_hbm, main, factor, halo_out, rim_out,
            x_left, x_right, edge_x, steps, t_high, t_low, keys, hot_a, hot_b, acc,
            rim_send, corner_send, rim_recv, corner_recv, il_recv, halo_send, halo_rim, halo_recv, halo_rim_recv,
            diag_recv, diag_corner, left_sem, right_sem, edge_sem, table_sem, send_sem, recv_sem):
    n_rows, n_cols, _ = x_left.shape
    span = LANES + x_right.shape[2]
    n_pairs, own_cols = n_rows // 2, n_cols // 2
    il, xl, ta = lax.axis_index("il"), lax.axis_index("xl"), lax.axis_index("ta")
    other = 1 - il
    has_xl, has_ta = (xl < n_xl - 1, xl > 0), (ta < n_ta - 1, ta > 0)
    xl_at, ta_at = (xl + 1, xl - 1), (ta + 1, ta - 1)
    ranges = column_ranges(n_cols)

    def when(condition, work):
        pl.when(condition)(work)

    step_load = pltpu.make_async_copy(steps_hbm, steps, table_sem.at[2])
    step_load.start()
    edge_loads = [pltpu.make_async_copy(traces.at[:, pl.ds(start, 8)], edge_x.at[d], edge_sem.at[d])
                  for d, start in enumerate((n_cols - 8, 0))]
    left_loads, right_loads = [], []
    for p in range(n_pairs):
        rows = pl.ds(2 * p, 2)
        left_loads.append(pltpu.make_async_copy(traces.at[rows, :, pl.ds(0, LANES)], x_left.at[rows], left_sem.at[p]))
        right_loads.append(pltpu.make_async_copy(traces.at[rows, :, pl.ds(LANES, span - LANES)], x_right.at[rows],
                                                 right_sem.at[p]))
    table_loads = [pltpu.make_async_copy(t_high_hbm, t_high, table_sem.at[0]),
                   pltpu.make_async_copy(t_low_hbm, t_low, table_sem.at[1])]
    for load in edge_loads:
        load.start()

    barrier = pltpu.get_barrier_semaphore()

    def greet(partner):
        pl.semaphore_signal(barrier, inc=1, device_id=partner, device_id_type=MESH)
        pl.semaphore_signal(barrier, inc=1, device_id={"il": other, **partner}, device_id_type=MESH)

    pl.semaphore_signal(barrier, inc=1, device_id={"il": other}, device_id_type=MESH)
    for d in range(2):
        when(has_ta[d], lambda d=d: greet({"ta": ta_at[d]}))
        when(has_xl[d], lambda d=d: greet({"xl": xl_at[d]}))
    for d in range(2):
        for e in range(2):
            when(has_xl[d] & has_ta[e], lambda d=d, e=e: greet({"xl": xl_at[d], "ta": ta_at[e]}))
    count_xl = sum(jnp.where(has, 1, 0) for has in has_xl)
    count_ta = sum(jnp.where(has, 1, 0) for has in has_ta)
    peers = 2 * (1 + count_xl) * (1 + count_ta) - 1
    for load in left_loads + right_loads + table_loads:
        load.start()

    for e in range(2):
        def no_ta(e=e):
            halo_recv[e] = jnp.zeros_like(halo_recv[e])
            halo_rim_recv[e] = jnp.zeros_like(halo_rim_recv[e])
        when(jnp.logical_not(has_ta[1 - e]), no_ta)
    for d in range(2):
        def no_xl(d=d):
            rim_recv[d] = jnp.zeros_like(rim_recv[d])
            corner_recv[d] = jnp.zeros_like(corner_recv[d])
        when(jnp.logical_not(has_xl[1 - d]), no_xl)
        for e in range(2):
            def no_diag(d=d, e=e):
                diag_recv[d, e] = jnp.zeros_like(diag_recv[d, e])
                diag_corner[d, e] = jnp.zeros_like(diag_corner[d, e])
            when(jnp.logical_not(has_xl[1 - d] & has_ta[1 - e]), no_diag)

    lane = lax.broadcasted_iota(jnp.int32, (1, LANES), 1)
    is_first, is_last = lane < REACH, lane >= LANES - REACH
    step_load.wait()
    col = lax.broadcasted_iota(jnp.int32, (n_rows, n_cols), 1)
    row = lax.broadcasted_iota(jnp.int32, (n_rows, n_cols), 0)
    bin_col = lax.shift_right_logical(col, 1) + steps[1]
    bin_row = steps[0] + 1
    own = (bin_col >= 0) & (bin_col < own_cols)
    code_a, code_b = [jnp.where(own, bin_row * height + bin_col - first, -1)[:, start:stop]
                      for start, stop, first, height in ranges]
    rest = n_cols - LANES
    keys[0] = code_a
    padded = jnp.concatenate([code_b, jnp.full((n_rows, LANES - rest), -1, jnp.int32)], axis=1)
    keys[1] = padded
    keys[2] = pltpu.roll(padded, rest, 1)

    def one_hot(key, height):
        rows = lax.broadcasted_iota(jnp.int32, (height, key.shape[1]), 0)
        return jnp.where(rows == key, 1.0, 0.0).astype(BF16)

    rim_bin = bin_row - 1 + lax.shift_right_logical(row, 1)
    outside = jnp.where(il == 0, n_pairs, -1)
    rim_code = jnp.where(rim_bin == outside, n_pairs, jnp.where((rim_bin < 0) | (rim_bin >= n_pairs), -1, rim_bin))
    for load in edge_loads:
        load.wait()
    for d, (start, column) in enumerate(((n_cols - 8, own_cols), (0, -1))):
        target = jnp.where(bin_col == column, rim_code, -1)
        key = jnp.concatenate([target[i: i + 1, start: start + 8] for i in range(n_rows)], axis=1)
        chosen = one_hot(key, n_pairs + 8)
        high, low = halves(edge_x[d].reshape(n_rows * 8, span))
        sums = dot(chosen, high) + dot(chosen, low)
        folds = dot(chosen, jnp.ones((n_rows * 8, LANES), BF16))
        ends = jnp.where(is_first, sums[:, :LANES], jnp.where(is_last, sums[:, span - LANES:], folds))
        rim_send[d, :, :span] = sums[:n_pairs]
        rim_send[d, :, span:] = ends[:n_pairs]
        corner_send[d, :, :span] = sums[n_pairs: n_pairs + 1]
        corner_send[d, :, span:] = ends[n_pairs: n_pairs + 1]

    for p in range(n_pairs):
        key = jnp.concatenate([keys[0, 2 * p: 2 * p + 1], keys[0, 2 * p + 1: 2 * p + 2]], axis=1)
        hot_a[p] = one_hot(key, 3 * ranges[0][3])
        second = keys[2, 2 * p + 1: 2 * p + 2]
        key = jnp.concatenate([jnp.where(lane < rest, keys[1, 2 * p: 2 * p + 1], second),
                               second[:, :2 * rest - LANES]], axis=1)
        hot_b[p] = one_hot(key, 3 * ranges[1][3])
    hots = (hot_a, hot_b)

    def merge(p, parts, lanes):
        (_, _, _, height), (_, _, first, rest_height) = ranges
        for r in range(3):
            a = parts[0][r * height: (r + 1) * height]
            b = parts[1][r * rest_height: (r + 1) * rest_height]
            both = a[first:] + b[: height - first]
            for at, part in ((0, a[:first]), (first, both), (height, b[height - first:])):
                where = (p + r, slice(at, at + part.shape[0]), lanes)
                acc[where] = part if p == 0 or r == 2 else acc[where] + part

    def bin_pair(p, x, lanes):
        parts, wide = [], x.shape[2]
        for hot, (start, stop, _, _) in zip(hots, ranges):
            high, low = halves(jnp.concatenate([x[2 * p, start:stop], x[2 * p + 1, start:stop]], axis=0))
            sums = dot(hot[p], jnp.concatenate([high, low], axis=1))
            parts.append(sums[:, :wide] + sums[:, wide:])
        merge(p, parts, lanes)

    def count_pair(p):
        parts = [dot(hot[p], jnp.ones((hot.shape[2], LANES), BF16)) for hot in hots]
        merge(p, parts, slice(span, span + LANES))

    def remote(src, dst, slot, partner):
        return pltpu.make_async_remote_copy(src_ref=src, dst_ref=dst, send_sem=send_sem.at[slot],
                                            recv_sem=recv_sem.at[slot], device_id=partner, device_id_type=MESH)

    rim_row = jnp.where(il == 0, n_pairs + 1, 0)
    own_row = jnp.where(il == 0, n_pairs - 1, 0)
    to_other = remote(acc.at[rim_row], il_recv, 0, {"il": other})
    rims, halos, diags = [], [], {}
    for d in range(2):
        rims.append((remote(rim_send.at[d], rim_recv.at[d], 1 + d, {"xl": xl_at[d]}),
                     remote(corner_send.at[d], corner_recv.at[d], 3 + d, {"il": other, "xl": xl_at[d]})))
        halos.append((remote(halo_send.at[d], halo_recv.at[d], 5 + d, {"ta": ta_at[d]}),
                      remote(halo_rim.at[d], halo_rim_recv.at[d], 7 + d, {"il": other, "ta": ta_at[d]})))
        for e in range(2):
            to, end = {"xl": xl_at[d], "ta": ta_at[e]}, pl.ds(span, LANES)
            diags[d, e] = (remote(rim_send.at[d, :, end], diag_recv.at[d, e], 9 + 2 * d + e, to),
                           remote(corner_send.at[d, :, end], diag_corner.at[d, e], 13 + 2 * d + e, {"il": other, **to}))

    def start_all(copies):
        for copy in copies:
            copy.start()

    def pack_halo(e):
        lanes = slice(0, LANES) if e else slice(span - LANES, span)
        rows = slice(0, REACH) if e else slice(LANES - REACH, LANES)
        for b in range(n_pairs):
            halo_send[e, b, :, :own_cols] = acc[b + 1, :, lanes].T[rows]
        halo_rim[e, :, :own_cols] = acc[rim_row, :, lanes].T[rows]

    pl.semaphore_wait(barrier, peers)
    for d in range(2):
        def go(d=d):
            start_all(rims[d])
            for e in range(2):
                when(has_ta[e], lambda e=e: start_all(diags[d, e]))
        when(has_xl[d], go)
    for load in left_loads:
        load.wait()
    for p in range(n_pairs):
        bin_pair(p, x_left, slice(0, LANES))
    pack_halo(1)
    when(has_ta[1], lambda: start_all(halos[1]))
    for load in right_loads:
        load.wait()
    for p in range(n_pairs):
        bin_pair(p, x_right, slice(LANES, span))
    pack_halo(0)
    when(has_ta[0], lambda: start_all(halos[0]))
    for p in range(n_pairs):
        count_pair(p)
    to_other.start()

    def resample(values):
        high, low = halves(values)
        return dot(high, t_high[...]) + (dot(low, t_high[...]) + dot(high, t_low[...]))

    for load in table_loads:
        load.wait()
    for i in range(n_pairs):
        b = jnp.where(il == 0, i, n_pairs - 1 - i)
        if i == n_pairs - 1:
            to_other.wait_recv()
            acc[b + 1] = acc[b + 1] + il_recv[...]
        main[b] = resample(acc[b + 1, :, :span])
    for d in range(2):
        def arrived(d=d):
            for copy in rims[d]:
                copy.wait_recv()
        when(has_xl[1 - d], arrived)
    sub = lax.broadcasted_iota(jnp.int32, (n_pairs, 1), 0)
    rim = jnp.concatenate([rim_recv[d] + jnp.where(sub == own_row, corner_recv[d], 0.0) for d in range(2)], axis=0)
    more = resample(rim[:, :span])
    more_fold = jnp.broadcast_to(rim[:, span + LANES // 2: span + LANES // 2 + 1], (2 * n_pairs, LANES))
    ends_row = lax.broadcasted_iota(jnp.int32, (8, 1), 0)
    tops = ((0, 0, 0), (own_cols - 8, 7, n_pairs))

    def add_rows(values, extra, b):
        top, bottom = [values[at: at + 8] + jnp.where(ends_row == where, extra[base + b: base + b + 1], 0.0)
                       for at, where, base in tops]
        return jnp.concatenate([top, values[8: own_cols - 8], bottom], axis=0)

    for b in range(n_pairs):
        scale = 1.0 / jnp.maximum(add_rows(acc[b + 1, :, span:], more_fold, b), 1.0)
        factor[b] = scale
        main[b] = add_rows(main[b], more, b) * jnp.concatenate([scale] * (main.shape[2] // LANES), axis=1)

    for d in range(2):
        for e in range(2):
            def diag_arrived(d=d, e=e):
                for copy in diags[d, e]:
                    copy.wait_recv()
            when(has_xl[1 - d] & has_ta[1 - e], diag_arrived)
    for d in range(2):
        first, last = [diag_recv[d, e] + jnp.where(sub == own_row, diag_corner[d, e], 0.0) for e in (1, 0)]
        rim_out[d * n_pairs: (d + 1) * n_pairs] = jnp.where(is_first, first, jnp.where(is_last, last, 0.0))
    for e in range(2):
        def halo_arrived(e=e):
            for copy in halos[e]:
                copy.wait_recv()
        when(has_ta[1 - e], halo_arrived)
        halo_out[e] = halo_recv[e]
        halo_out[e, own_row] = halo_recv[e, own_row] + halo_rim_recv[e]
    to_other.wait_send()
    for d in range(2):
        def sent(d=d):
            for copy in rims[d]:
                copy.wait_send()
            for e in range(2):
                def diag_sent(d=d, e=e):
                    for copy in diags[d, e]:
                        copy.wait_send()
                when(has_ta[e], diag_sent)
        when(has_xl[d], sent)

        def halo_sent(d=d):
            for copy in halos[d]:
                copy.wait_send()
        when(has_ta[d], halo_sent)


def finish(main, factor, halo, rim, t_edge, t_rim, out, staged, out_sem):
    n_pairs, own_cols, width = main.shape
    inner = pl.ds(LANES, width - 2 * LANES)
    writes = [pltpu.make_async_copy(main.at[:, :, inner], out.at[:, :, inner], out_sem.at[n_pairs, 0])]
    writes[0].start()
    high = rim[...].astype(BF16)
    low = (rim[...] - high.astype(F32)).astype(BF16)
    more = dot(jnp.concatenate([high, low, high], axis=1), t_rim[...])
    ends_row = lax.broadcasted_iota(jnp.int32, (8, 1), 0)
    tops = ((0, 0, 0), (own_cols - 8, 7, n_pairs))
    for b in range(n_pairs):
        edges = jnp.concatenate([halo[0, b], halo[1, b]], axis=0)
        high = edges.astype(BF16).astype(F32)
        terms = jnp.concatenate([high, edges - high, high], axis=0).T[:own_cols].astype(BF16)
        ends = dot(terms, t_edge[...])
        top, bottom = [ends[at: at + 8] + jnp.where(ends_row == where, more[base + b: base + b + 1], 0.0)
                       for at, where, base in tops]
        ends = jnp.concatenate([top, ends[8: own_cols - 8], bottom], axis=0)
        for d, start in enumerate((0, width - LANES)):
            staged[b, d] = main[b, :, start: start + LANES] + ends[:, d * LANES: (d + 1) * LANES] * factor[b]
            write = pltpu.make_async_copy(staged.at[b, d], out.at[b, :, pl.ds(start, LANES)], out_sem.at[b, d])
            write.start()
            writes.append(write)
    for write in writes:
        write.wait()


def shards(n_xl, n_ta, traces, bin_steps):
    n_rows, n_cols, span = traces.shape
    n_pairs, own_cols = n_rows // 2, n_cols // 2
    width = span + LANES
    out_span = span * P_SIZE // Q
    if n_pairs % 8 or span % LANES or out_span % LANES or out_span < 3 * LANES:
        raise ValueError("block shape")
    table = lanczos_table(span)
    t_high, t_low = split_table(table[REACH:-REACH])
    edge_cols = np.concatenate([table[:, :LANES], table[:, -LANES:]], axis=1)
    edge_high, edge_low = split_table(np.concatenate([edge_cols[:REACH], edge_cols[-REACH:]]))
    t_edge = np.concatenate([edge_high, edge_high, edge_low])
    rim_high, rim_low = split_table(np.concatenate(
        [edge_cols[-REACH:], np.zeros((LANES - 2 * REACH, 2 * LANES), np.float32), edge_cols[:REACH]]))
    t_rim = np.concatenate([rim_high, rim_high, rim_low])
    vmem = pl.BlockSpec(memory_space=pltpu.VMEM)
    hbm = pl.BlockSpec(memory_space=pltpu.HBM)
    (start_a, stop_a, _, height_a), (start_b, stop_b, _, height_b) = column_ranges(n_cols)
    main, factor, halo, rim = pl.pallas_call(
        functools.partial(binning, n_xl, n_ta),
        out_shape=(pltpu.VMEM((n_pairs, own_cols, out_span), F32), pltpu.VMEM((n_pairs, own_cols, LANES), F32),
                   pltpu.VMEM((2, n_pairs, REACH, LANES), F32), pltpu.VMEM((2 * n_pairs, LANES), F32)),
        in_specs=[hbm] * 4,
        out_specs=[vmem] * 4,
        scratch_shapes=[
            pltpu.VMEM((n_rows, n_cols, LANES), F32),
            pltpu.VMEM((n_rows, n_cols, span - LANES), F32),
            pltpu.VMEM((2, n_rows, 8, span), F32),
            pltpu.VMEM((2, n_rows, n_cols), jnp.int32),
            pltpu.VMEM(t_high.shape, BF16),
            pltpu.VMEM(t_low.shape, BF16),
            pltpu.VMEM((3, n_rows, LANES), jnp.int32),
            pltpu.VMEM((n_pairs, 3 * height_a, 2 * (stop_a - start_a)), BF16),
            pltpu.VMEM((n_pairs, 3 * height_b, 2 * (stop_b - start_b)), BF16),
            pltpu.VMEM((n_pairs + 2, own_cols, width), F32),
            pltpu.VMEM((2, n_pairs, width), F32),
            pltpu.VMEM((2, 1, width), F32),
            pltpu.VMEM((2, n_pairs, width), F32),
            pltpu.VMEM((2, 1, width), F32),
            pltpu.VMEM((own_cols, width), F32),
            pltpu.VMEM((2, n_pairs, REACH, LANES), F32),
            pltpu.VMEM((2, REACH, LANES), F32),
            pltpu.VMEM((2, n_pairs, REACH, LANES), F32),
            pltpu.VMEM((2, REACH, LANES), F32),
            pltpu.VMEM((2, 2, n_pairs, LANES), F32),
            pltpu.VMEM((2, 2, 1, LANES), F32),
            pltpu.SemaphoreType.DMA((n_pairs,)),
            pltpu.SemaphoreType.DMA((n_pairs,)),
            pltpu.SemaphoreType.DMA((2,)),
            pltpu.SemaphoreType.DMA((3,)),
            pltpu.SemaphoreType.DMA((17,)),
            pltpu.SemaphoreType.DMA((17,)),
        ],
        compiler_params=pltpu.CompilerParams(collective_id=0, has_side_effects=True, vmem_limit_bytes=24 * 2**20),
        name="binning",
    )(*[pltpu.with_memory_space_constraint(a, pltpu.HBM) for a in (traces, bin_steps, jnp.asarray(t_high), jnp.asarray(t_low))])
    return pl.pallas_call(
        finish,
        out_shape=jax.ShapeDtypeStruct((n_pairs, own_cols, out_span), F32),
        in_specs=[vmem] * 6,
        out_specs=hbm,
        scratch_shapes=[pltpu.VMEM((n_pairs, 2, own_cols, LANES), F32), pltpu.SemaphoreType.DMA((n_pairs + 1, 2))],
        compiler_params=pltpu.CompilerParams(vmem_limit_bytes=16 * 2**20),
        name="finish",
    )(main, factor, halo, rim, jnp.asarray(t_edge), jnp.asarray(t_rim))


def solution(mesh):
    if mesh.shape["il"] != 2:
        raise ValueError("il size")
    return jax.shard_map(
        functools.partial(shards, mesh.shape["xl"], mesh.shape["ta"]),
        mesh=mesh,
        in_specs=(P("il", "xl", "ta"), P(None, "il", "xl")),
        out_specs=P("il", "xl", "ta"),
        check_vma=False,
    )
```

time: 11.9 us -> 10.2 us (0.86)
  Pallas kernels: 11.7 us -> 10.1 us
    pallas_call x1, Pallas kernels: 10.4 us -> 8.78 us  [shards(): pl.pallas_call(functools.partial(binning, n_xl, n_ta), out_shape=(pltpu.V...]
where the time goes in v1:
time: 10.2 us; the launch traced here: 10.1 us
  Pallas kernels  10.1 us (99%)
    pallas_call x1, Pallas kernels, shards(): pl.pallas_call(functools.partial(binning, n_xl, n_ta), out_shape=(pltpu.V...  8.78 us
    pallas_call x1, Pallas kernels, shards(): pl.pallas_call(finish, out_shape=jax.ShapeDtypeStruct((n_pairs, own_cols,...  1.27 us

profile of v1, /device:TPU:0, one launch (start us, length us, event | category | flops | bytes accessed | tf_op | source)
XLA Modules:
  0.0 10.1 jit_solution(12064308332816026023)
XLA Ops:
  0.0 0.0 copy-start
  0.0 0.0 copy-start.1
  0.0 8.8 %binning.1 = (f32[8,104,384]{2,1,0:T(8,128)S(1)}, f32[8,104,128]{2,1,0:T(8,128)S(1)}, f32[2,8,8,128]{3,2,1,0:T(8,128)S(1)}, f32[16,128]{1,0:T(8,128)S(1)}) custom-call(f32[16,208,256]{2,1,0:T(8,128)} %traces.1, s32[2,16,208]{2,1,0:T(8,128)} %steps_hbm.1, bf16[256,384]{1,0:T(8,128)(2,1)} %constant.8.clone.t_high_hbm, bf16[256,384]{1,0:T(8,128)(2,1)} %constant.9.clone.t_low_hbm), custom_call_target="tpu_custom_call" | custom-call | tf_op jit(solution)/shard_map/binning/pallas_call | solution.py:353
  8.8 0.0 copy-done
  8.8 0.0 copy-done.1
  8.8 1.3 %finish.1 = f32[8,104,384]{2,1,0:T(8,128)} custom-call(f32[8,104,384]{2,1,0:T(8,128)S(1)} %get-tuple-element.9.main, f32[8,104,128]{2,1,0:T(8,128)S(1)} %get-tuple-element.10.factor, f32[2,8,8,128]{3,2,1,0:T(8,128)S(1)} %get-tuple-element.11.halo, f32[16,128]{1,0:T(8,128)S(1)} %get-tuple-element.12.rim, bf16[48,256]{1,0:T(8,128)(2,1)S(1)} %copy-done.1, ...), custom_call_target="tpu_custom_call" | custom-call | tf_op jit(solution)/shard_map/finish/pallas_call | solution.py:391
Async XLA Ops:
  0.0 8.8 %copy-start = (bf16[384,256]{1,0:T(8,128)(2,1)S(1)}, bf16[384,256]{1,0:T(8,128)(2,1)}, u32[]{:S(2)}) copy-start(bf16[384,256]{1,0:T(8,128)(2,1)} %constant.11.clone.t_rim) | copy-start | bytes 589828
  0.0 8.8 %copy-start.1 = (bf16[48,256]{1,0:T(8,128)(2,1)S(1)}, bf16[48,256]{1,0:T(8,128)(2,1)}, u32[]{:S(2)}) copy-start(bf16[48,256]{1,0:T(8,128)(2,1)} %constant.10.clone.t_edge) | copy-start | bytes 73732

commit v2 on v1

--- a/solution.py
+++ b/solution.py
@@ -13,6 +13,7 @@
 Q = 2
 REACH = TAPS // 2
 LANES = 128
+EARLY = 2
 MESH = pl.DeviceIdType.MESH
 F32, BF16 = jnp.float32, jnp.bfloat16
 
@@ -50,10 +51,10 @@
     return (0, LANES, 0, height), (LANES, n_cols, first, own_cols - first)
 
 
-def binning(n_xl, n_ta, traces, steps_hbm, t_high_hbm, t_low_hbm, main, factor, halo_out, rim_out,
-            x_left, x_right, edge_x, steps, t_high, t_low, keys, hot_a, hot_b, acc,
+def binning(n_xl, n_ta, traces, steps_hbm, tables_hbm, main, factor, halo_out, rim_out,
+            x_left, x_right, edge_x, steps, tables, keys, hot_a, hot_b, acc,
             rim_send, corner_send, rim_recv, corner_recv, il_recv, halo_send, halo_rim, halo_recv, halo_rim_recv,
-            diag_recv, diag_corner, left_sem, right_sem, edge_sem, table_sem, send_sem, recv_sem):
+            diag_recv, diag_corner, load_sem, late_sem, send_sem, recv_sem):
     n_rows, n_cols, _ = x_left.shape
     span = LANES + x_right.shape[2]
     n_pairs, own_cols = n_rows // 2, n_cols // 2
@@ -66,39 +67,37 @@
     def when(condition, work):
         pl.when(condition)(work)
 
-    step_load = pltpu.make_async_copy(steps_hbm, steps, table_sem.at[2])
+    step_load = pltpu.make_async_copy(steps_hbm, steps, load_sem.at[3])
     step_load.start()
-    edge_loads = [pltpu.make_async_copy(traces.at[:, pl.ds(start, 8)], edge_x.at[d], edge_sem.at[d])
+    edge_loads = [pltpu.make_async_copy(traces.at[:, pl.ds(start, 8)], edge_x.at[d], load_sem.at[4 + d])
                   for d, start in enumerate((n_cols - 8, 0))]
-    left_loads, right_loads = [], []
-    for p in range(n_pairs):
-        rows = pl.ds(2 * p, 2)
-        left_loads.append(pltpu.make_async_copy(traces.at[rows, :, pl.ds(0, LANES)], x_left.at[rows], left_sem.at[p]))
-        right_loads.append(pltpu.make_async_copy(traces.at[rows, :, pl.ds(LANES, span - LANES)], x_right.at[rows],
-                                                 right_sem.at[p]))
-    table_loads = [pltpu.make_async_copy(t_high_hbm, t_high, table_sem.at[0]),
-                   pltpu.make_async_copy(t_low_hbm, t_low, table_sem.at[1])]
     for load in edge_loads:
         load.start()
 
+    def load_samples(x, start, rows, slot):
+        samples = pl.ds(start, x.shape[2])
+        return pltpu.make_async_copy(traces.at[rows, :, samples], x.at[rows], load_sem.at[slot])
+
+    table_load = pltpu.make_async_copy(tables_hbm, tables, load_sem.at[2])
+
     barrier = pltpu.get_barrier_semaphore()
 
-    def greet(partner):
-        pl.semaphore_signal(barrier, inc=1, device_id=partner, device_id_type=MESH)
-        pl.semaphore_signal(barrier, inc=1, device_id={"il": other, **partner}, device_id_type=MESH)
+    def greet(has, partner, semaphore=barrier):
+        def signal():
+            pl.semaphore_signal(semaphore, inc=1, device_id=partner, device_id_type=MESH)
+            pl.semaphore_signal(semaphore, inc=1, device_id={"il": other, **partner}, device_id_type=MESH)
+        when(has, signal)
 
     pl.semaphore_signal(barrier, inc=1, device_id={"il": other}, device_id_type=MESH)
     for d in range(2):
-        when(has_ta[d], lambda d=d: greet({"ta": ta_at[d]}))
-        when(has_xl[d], lambda d=d: greet({"xl": xl_at[d]}))
-    for d in range(2):
-        for e in range(2):
-            when(has_xl[d] & has_ta[e], lambda d=d, e=e: greet({"xl": xl_at[d], "ta": ta_at[e]}))
-    count_xl = sum(jnp.where(has, 1, 0) for has in has_xl)
-    count_ta = sum(jnp.where(has, 1, 0) for has in has_ta)
-    peers = 2 * (1 + count_xl) * (1 + count_ta) - 1
-    for load in left_loads + right_loads + table_loads:
-        load.start()
+        greet(has_xl[0] & has_ta[d], {"xl": xl + 1, "ta": ta_at[d]})
+    for d in range(2):
+        greet(has_xl[d], {"xl": xl_at[d]})
+        greet(has_ta[d], {"ta": ta_at[d]})
+    count_xl, count_ta = [sum(jnp.where(has, 1, 0) for has in pair) for pair in (has_xl, has_ta)]
+    peers = 1 + 2 * (count_xl + count_ta + jnp.where(has_xl[1], count_ta, 0))
+    for p in range(n_pairs):
+        load_samples(x_left, 0, pl.ds(2 * p, 2), 0).start()
 
     for e in range(2):
         def no_ta(e=e):
@@ -155,6 +154,9 @@
         corner_send[d, :, span:] = ends[n_pairs: n_pairs + 1]
 
     for p in range(n_pairs):
+        load_samples(x_right, LANES, pl.ds(2 * p, 2), 1).start()
+    table_load.start()
+    for p in range(n_pairs):
         key = jnp.concatenate([keys[0, 2 * p: 2 * p + 1], keys[0, 2 * p + 1: 2 * p + 2]], axis=1)
         hot_a[p] = one_hot(key, 3 * ranges[0][3])
         second = keys[2, 2 * p + 1: 2 * p + 2]
@@ -214,35 +216,51 @@
             halo_send[e, b, :, :own_cols] = acc[b + 1, :, lanes].T[rows]
         halo_rim[e, :, :own_cols] = acc[rim_row, :, lanes].T[rows]
 
+    def send_diags(d):
+        for e in (1, 0):
+            when(has_ta[e], lambda e=e: start_all(diags[d, e]))
+
+    def send_rims(d):
+        send_diags(d)
+        start_all(rims[d])
+
+    every_row = pl.ds(0, n_rows)
+    load_samples(x_left, 0, every_row, 0).wait()
+    for p in range(EARLY):
+        bin_pair(p, x_left, slice(0, LANES))
     pl.semaphore_wait(barrier, peers)
-    for d in range(2):
-        def go(d=d):
-            start_all(rims[d])
-            for e in range(2):
-                when(has_ta[e], lambda e=e: start_all(diags[d, e]))
-        when(has_xl[d], go)
-    for load in left_loads:
-        load.wait()
-    for p in range(n_pairs):
+    for e in range(2):
+        greet(has_ta[e], {"ta": ta_at[e]}, late_sem)
+    when(has_xl[1], lambda: send_rims(1))
+    when(has_xl[0], lambda: start_all(rims[0]))
+    for p in range(EARLY, n_pairs):
         bin_pair(p, x_left, slice(0, LANES))
     pack_halo(1)
     when(has_ta[1], lambda: start_all(halos[1]))
-    for load in right_loads:
-        load.wait()
-    for p in range(n_pairs):
+    load_samples(x_right, LANES, every_row, 1).wait()
+    for p in range(n_pairs // 2):
+        bin_pair(p, x_right, slice(LANES, span))
+
+    def late():
+        pl.semaphore_wait(late_sem, 2 * count_ta)
+        when(has_xl[0], lambda: send_diags(0))
+
+    first = (xl == 0) & (ta == 0)
+    when(jnp.logical_not(first), late)
+    for p in range(n_pairs // 2, n_pairs):
         bin_pair(p, x_right, slice(LANES, span))
     pack_halo(0)
     when(has_ta[0], lambda: start_all(halos[0]))
     for p in range(n_pairs):
         count_pair(p)
     to_other.start()
+    when(first, late)
 
     def resample(values):
         high, low = halves(values)
-        return dot(high, t_high[...]) + (dot(low, t_high[...]) + dot(high, t_low[...]))
-
-    for load in table_loads:
-        load.wait()
+        return dot(high, tables[0]) + (dot(low, tables[0]) + dot(high, tables[1]))
+
+    table_load.wait()
     for i in range(n_pairs):
         b = jnp.where(il == 0, i, n_pairs - 1 - i)
         if i == n_pairs - 1:
@@ -308,7 +326,7 @@
 def finish(main, factor, halo, rim, t_edge, t_rim, out, staged, out_sem):
     n_pairs, own_cols, width = main.shape
     inner = pl.ds(LANES, width - 2 * LANES)
-    writes = [pltpu.make_async_copy(main.at[:, :, inner], out.at[:, :, inner], out_sem.at[n_pairs, 0])]
+    writes = [pltpu.make_async_copy(main.at[:, :, inner], out.at[:, :, inner], out_sem.at[0])]
     writes[0].start()
     high = rim[...].astype(BF16)
     low = (rim[...] - high.astype(F32)).astype(BF16)
@@ -325,11 +343,11 @@
         ends = jnp.concatenate([top, ends[8: own_cols - 8], bottom], axis=0)
         for d, start in enumerate((0, width - LANES)):
             staged[b, d] = main[b, :, start: start + LANES] + ends[:, d * LANES: (d + 1) * LANES] * factor[b]
-            write = pltpu.make_async_copy(staged.at[b, d], out.at[b, :, pl.ds(start, LANES)], out_sem.at[b, d])
+            write = pltpu.make_async_copy(staged.at[b, d], out.at[b, :, pl.ds(start, LANES)], out_sem.at[1])
             write.start()
-            writes.append(write)
-    for write in writes:
-        write.wait()
+    writes[0].wait()
+    for d, start in enumerate((0, width - LANES)):
+        pltpu.make_async_copy(staged.at[:, d], out.at[:, :, pl.ds(start, LANES)], out_sem.at[1]).wait()
 
 
 def shards(n_xl, n_ta, traces, bin_steps):
@@ -340,7 +358,7 @@
     if n_pairs % 8 or span % LANES or out_span % LANES or out_span < 3 * LANES:
         raise ValueError("block shape")
     table = lanczos_table(span)
-    t_high, t_low = split_table(table[REACH:-REACH])
+    tables = np.stack(split_table(table[REACH:-REACH]))
     edge_cols = np.concatenate([table[:, :LANES], table[:, -LANES:]], axis=1)
     edge_high, edge_low = split_table(np.concatenate([edge_cols[:REACH], edge_cols[-REACH:]]))
     t_edge = np.concatenate([edge_high, edge_high, edge_low])
@@ -354,15 +372,14 @@
         functools.partial(binning, n_xl, n_ta),
         out_shape=(pltpu.VMEM((n_pairs, own_cols, out_span), F32), pltpu.VMEM((n_pairs, own_cols, LANES), F32),
                    pltpu.VMEM((2, n_pairs, REACH, LANES), F32), pltpu.VMEM((2 * n_pairs, LANES), F32)),
-        in_specs=[hbm] * 4,
+        in_specs=[hbm] * 3,
         out_specs=[vmem] * 4,
         scratch_shapes=[
             pltpu.VMEM((n_rows, n_cols, LANES), F32),
             pltpu.VMEM((n_rows, n_cols, span - LANES), F32),
             pltpu.VMEM((2, n_rows, 8, span), F32),
             pltpu.VMEM((2, n_rows, n_cols), jnp.int32),
-            pltpu.VMEM(t_high.shape, BF16),
-            pltpu.VMEM(t_low.shape, BF16),
+            pltpu.VMEM(tables.shape, BF16),
             pltpu.VMEM((3, n_rows, LANES), jnp.int32),
             pltpu.VMEM((n_pairs, 3 * height_a, 2 * (stop_a - start_a)), BF16),
             pltpu.VMEM((n_pairs, 3 * height_b, 2 * (stop_b - start_b)), BF16),
@@ -378,22 +395,20 @@
             pltpu.VMEM((2, REACH, LANES), F32),
             pltpu.VMEM((2, 2, n_pairs, LANES), F32),
             pltpu.VMEM((2, 2, 1, LANES), F32),
-            pltpu.SemaphoreType.DMA((n_pairs,)),
-            pltpu.SemaphoreType.DMA((n_pairs,)),
-            pltpu.SemaphoreType.DMA((2,)),
-            pltpu.SemaphoreType.DMA((3,)),
+            pltpu.SemaphoreType.DMA((6,)),
+            pltpu.SemaphoreType.REGULAR,
             pltpu.SemaphoreType.DMA((17,)),
             pltpu.SemaphoreType.DMA((17,)),
         ],
         compiler_params=pltpu.CompilerParams(collective_id=0, has_side_effects=True, vmem_limit_bytes=24 * 2**20),
         name="binning",
-    )(*[pltpu.with_memory_space_constraint(a, pltpu.HBM) for a in (traces, bin_steps, jnp.asarray(t_high), jnp.asarray(t_low))])
+    )(*[pltpu.with_memory_space_constraint(a, pltpu.HBM) for a in (traces, bin_steps, jnp.asarray(tables))])
     return pl.pallas_call(
         finish,
         out_shape=jax.ShapeDtypeStruct((n_pairs, own_cols, out_span), F32),
         in_specs=[vmem] * 6,
         out_specs=hbm,
-        scratch_shapes=[pltpu.VMEM((n_pairs, 2, own_cols, LANES), F32), pltpu.SemaphoreType.DMA((n_pairs + 1, 2))],
+        scratch_shapes=[pltpu.VMEM((n_pairs, 2, own_cols, LANES), F32), pltpu.SemaphoreType.DMA((2,))],
         compiler_params=pltpu.CompilerParams(vmem_limit_bytes=16 * 2**20),
         name="finish",
     )(main, factor, halo, rim, jnp.asarray(t_edge), jnp.asarray(t_rim))

time: 10.2 us -> 9.6 us (0.941)
  the two profiles are of different devices: /device:TPU:0 before, /device:TPU:5 now
where the time goes in v2:
time: 9.6 us; the launch traced here: 9.46 us
  Pallas kernels  9.43 us (98%)
    pallas_call x1, Pallas kernels, shards(): pl.pallas_call(functools.partial(binning, n_xl, n_ta), out_shape=(pltpu.V...  8.3 us
    pallas_call x1, Pallas kernels, shards(): pl.pallas_call(finish, out_shape=jax.ShapeDtypeStruct((n_pairs, own_cols,...  1.13 us

profile of v2, /device:TPU:5, one launch (start us, length us, event | category | flops | bytes accessed | tf_op | source)
XLA Modules:
  0.0 9.5 jit_solution(14674696118406568532)
XLA Ops:
  0.0 0.0 copy-start
  0.0 0.0 copy-start.1
  0.0 8.3 %binning.1 = (f32[8,104,384]{2,1,0:T(8,128)S(1)}, f32[8,104,128]{2,1,0:T(8,128)S(1)}, f32[2,8,8,128]{3,2,1,0:T(8,128)S(1)}, f32[16,128]{1,0:T(8,128)S(1)}) custom-call(f32[16,208,256]{2,1,0:T(8,128)} %traces.1, s32[2,16,208]{2,1,0:T(8,128)} %steps_hbm.1, bf16[2,256,384]{2,1,0:T(8,128)(2,1)} %constant.6.clone.tables_hbm), custom_call_target="tpu_custom_call" | custom-call | tf_op jit(solution)/shard_map/binning/pallas_call | solution.py:371
  8.3 0.0 copy-done
  8.3 0.0 copy-done.1
  8.3 1.1 %finish.1 = f32[8,104,384]{2,1,0:T(8,128)} custom-call(f32[8,104,384]{2,1,0:T(8,128)S(1)} %get-tuple-element.9.main, f32[8,104,128]{2,1,0:T(8,128)S(1)} %get-tuple-element.10.factor, f32[2,8,8,128]{3,2,1,0:T(8,128)S(1)} %get-tuple-element.11.halo, f32[16,128]{1,0:T(8,128)S(1)} %get-tuple-element.12.rim, bf16[48,256]{1,0:T(8,128)(2,1)S(1)} %copy-done.1, ...), custom_call_target="tpu_custom_call" | custom-call | tf_op jit(solution)/shard_map/finish/pallas_call | solution.py:406
Async XLA Ops:
  0.0 8.3 %copy-start = (bf16[384,256]{1,0:T(8,128)(2,1)S(1)}, bf16[384,256]{1,0:T(8,128)(2,1)}, u32[]{:S(2)}) copy-start(bf16[384,256]{1,0:T(8,128)(2,1)} %constant.8.clone.t_rim) | copy-start | bytes 589828
  0.0 8.3 %copy-start.1 = (bf16[48,256]{1,0:T(8,128)(2,1)S(1)}, bf16[48,256]{1,0:T(8,128)(2,1)}, u32[]{:S(2)}) copy-start(bf16[48,256]{1,0:T(8,128)(2,1)} %constant.7.clone.t_edge) | copy-start | bytes 73732

commit v3 on v2

--- a/solution.py
+++ b/solution.py
@@ -13,7 +13,6 @@
 Q = 2
 REACH = TAPS // 2
 LANES = 128
-EARLY = 2
 MESH = pl.DeviceIdType.MESH
 F32, BF16 = jnp.float32, jnp.bfloat16
 
@@ -53,7 +52,7 @@
 
 def binning(n_xl, n_ta, traces, steps_hbm, tables_hbm, main, factor, halo_out, rim_out,
             x_left, x_right, edge_x, steps, tables, keys, hot_a, hot_b, acc,
-            rim_send, corner_send, rim_recv, corner_recv, il_recv, halo_send, halo_rim, halo_recv, halo_rim_recv,
+            rim_send, corner_send, rim_recv, corner_recv, il_recv, halo_send, halo_recv, wide_rows,
             diag_recv, diag_corner, load_sem, late_sem, send_sem, recv_sem):
     n_rows, n_cols, _ = x_left.shape
     span = LANES + x_right.shape[2]
@@ -82,10 +81,10 @@
 
     barrier = pltpu.get_barrier_semaphore()
 
-    def greet(has, partner, semaphore=barrier):
+    def greet(has, partner):
         def signal():
-            pl.semaphore_signal(semaphore, inc=1, device_id=partner, device_id_type=MESH)
-            pl.semaphore_signal(semaphore, inc=1, device_id={"il": other, **partner}, device_id_type=MESH)
+            pl.semaphore_signal(barrier, inc=1, device_id=partner, device_id_type=MESH)
+            pl.semaphore_signal(barrier, inc=1, device_id={"il": other, **partner}, device_id_type=MESH)
         when(has, signal)
 
     pl.semaphore_signal(barrier, inc=1, device_id={"il": other}, device_id_type=MESH)
@@ -102,7 +101,6 @@
     for e in range(2):
         def no_ta(e=e):
             halo_recv[e] = jnp.zeros_like(halo_recv[e])
-            halo_rim_recv[e] = jnp.zeros_like(halo_rim_recv[e])
         when(jnp.logical_not(has_ta[1 - e]), no_ta)
     for d in range(2):
         def no_xl(d=d):
@@ -154,9 +152,6 @@
         corner_send[d, :, span:] = ends[n_pairs: n_pairs + 1]
 
     for p in range(n_pairs):
-        load_samples(x_right, LANES, pl.ds(2 * p, 2), 1).start()
-    table_load.start()
-    for p in range(n_pairs):
         key = jnp.concatenate([keys[0, 2 * p: 2 * p + 1], keys[0, 2 * p + 1: 2 * p + 2]], axis=1)
         hot_a[p] = one_hot(key, 3 * ranges[0][3])
         second = keys[2, 2 * p + 1: 2 * p + 2]
@@ -164,16 +159,20 @@
                                second[:, :2 * rest - LANES]], axis=1)
         hot_b[p] = one_hot(key, 3 * ranges[1][3])
     hots = (hot_a, hot_b)
-
-    def merge(p, parts, lanes):
-        (_, _, _, height), (_, _, first, rest_height) = ranges
-        for r in range(3):
-            a = parts[0][r * height: (r + 1) * height]
-            b = parts[1][r * rest_height: (r + 1) * rest_height]
-            both = a[first:] + b[: height - first]
-            for at, part in ((0, a[:first]), (first, both), (height, b[height - first:])):
-                where = (p + r, slice(at, at + part.shape[0]), lanes)
-                acc[where] = part if p == 0 or r == 2 else acc[where] + part
+    for p in range(n_pairs):
+        load_samples(x_right, LANES, pl.ds(2 * p, 2), 1).start()
+    table_load.start()
+
+    def merge(p, r, parts, lanes):
+        (_, _, _, height), (_, _, first, _) = ranges
+        a, b = parts
+        both = a[first:] + b[: height - first]
+        for at, part in ((0, a[:first]), (first, both), (height, b[height - first:])):
+            where = (p + r, slice(at, at + part.shape[0]), lanes)
+            acc[where] = part if p == 0 or r == 2 else acc[where] + part
+
+    def groups(parts, r):
+        return [part[r * height: (r + 1) * height] for part, (_, _, _, height) in zip(parts, ranges)]
 
     def bin_pair(p, x, lanes):
         parts, wide = [], x.shape[2]
@@ -181,11 +180,16 @@
             high, low = halves(jnp.concatenate([x[2 * p, start:stop], x[2 * p + 1, start:stop]], axis=0))
             sums = dot(hot[p], jnp.concatenate([high, low], axis=1))
             parts.append(sums[:, :wide] + sums[:, wide:])
-        merge(p, parts, lanes)
+        for r in range(3):
+            merge(p, r, groups(parts, r), lanes)
+
+    ends = (0, 0), (n_pairs - 1, 2)
 
     def count_pair(p):
         parts = [dot(hot[p], jnp.ones((hot.shape[2], LANES), BF16)) for hot in hots]
-        merge(p, parts, slice(span, span + LANES))
+        for r in range(3):
+            if (p, r) not in ends:
+                merge(p, r, groups(parts, r), slice(span, span + LANES))
 
     def remote(src, dst, slot, partner):
         return pltpu.make_async_remote_copy(src_ref=src, dst_ref=dst, send_sem=send_sem.at[slot],
@@ -194,16 +198,31 @@
     rim_row = jnp.where(il == 0, n_pairs + 1, 0)
     own_row = jnp.where(il == 0, n_pairs - 1, 0)
     to_other = remote(acc.at[rim_row], il_recv, 0, {"il": other})
+
     rims, halos, diags = [], [], {}
     for d in range(2):
-        rims.append((remote(rim_send.at[d], rim_recv.at[d], 1 + d, {"xl": xl_at[d]}),
-                     remote(corner_send.at[d], corner_recv.at[d], 3 + d, {"il": other, "xl": xl_at[d]})))
-        halos.append((remote(halo_send.at[d], halo_recv.at[d], 5 + d, {"ta": ta_at[d]}),
-                      remote(halo_rim.at[d], halo_rim_recv.at[d], 7 + d, {"il": other, "ta": ta_at[d]})))
+        to, rows = {"xl": xl_at[d]}, pl.ds(0, n_pairs)
+        rims.append((remote(rim_send.at[d], rim_recv.at[d], 1 + d, to),
+                     remote(corner_send.at[d], corner_recv.at[d], 1 + d, {"il": other, **to})))
+        to = {"ta": ta_at[d]}
+        halos.append((remote(halo_send.at[d, rows], halo_recv.at[d, rows], 3 + d, to),
+                      remote(halo_send.at[d, n_pairs], halo_recv.at[d, n_pairs], 3 + d, {"il": other, **to})))
         for e in range(2):
-            to, end = {"xl": xl_at[d], "ta": ta_at[e]}, pl.ds(span, LANES)
-            diags[d, e] = (remote(rim_send.at[d, :, end], diag_recv.at[d, e], 9 + 2 * d + e, to),
-                           remote(corner_send.at[d, :, end], diag_corner.at[d, e], 13 + 2 * d + e, {"il": other, **to}))
+            to, end, slot = {"xl": xl_at[d], "ta": ta_at[e]}, pl.ds(span, LANES), 5 + 2 * d + e
+            diags[d, e] = (remote(rim_send.at[d, :, end], diag_recv.at[d, e], slot, to),
+                           remote(corner_send.at[d, :, end], diag_corner.at[d, e], slot, {"il": other, **to}))
+
+    def wait_all(semaphores, slot, rows):
+        pltpu.make_async_copy(rows, rows, semaphores.at[slot]).wait()
+
+    def wait_rims(semaphores, d):
+        wait_all(semaphores, 1 + d, wide_rows)
+
+    def wait_halos(semaphores, e):
+        wait_all(semaphores, 3 + e, halo_recv.at[e])
+
+    def wait_diags(semaphores, d, e):
+        wait_all(semaphores, 5 + 2 * d + e, wide_rows.at[:, :, pl.ds(0, LANES)])
 
     def start_all(copies):
         for copy in copies:
@@ -214,7 +233,7 @@
         rows = slice(0, REACH) if e else slice(LANES - REACH, LANES)
         for b in range(n_pairs):
             halo_send[e, b, :, :own_cols] = acc[b + 1, :, lanes].T[rows]
-        halo_rim[e, :, :own_cols] = acc[rim_row, :, lanes].T[rows]
+        halo_send[e, n_pairs, :, :own_cols] = acc[rim_row, :, lanes].T[rows]
 
     def send_diags(d):
         for e in (1, 0):
@@ -224,37 +243,40 @@
         send_diags(d)
         start_all(rims[d])
 
+    def late(e):
+        def go():
+            pl.semaphore_wait(late_sem.at[e], 1)
+            when(has_xl[0], lambda: start_all(diags[0, e]))
+        when(has_ta[e], go)
+
     every_row = pl.ds(0, n_rows)
-    load_samples(x_left, 0, every_row, 0).wait()
-    for p in range(EARLY):
-        bin_pair(p, x_left, slice(0, LANES))
     pl.semaphore_wait(barrier, peers)
     for e in range(2):
-        greet(has_ta[e], {"ta": ta_at[e]}, late_sem)
+        when(has_ta[e], lambda e=e: pl.semaphore_signal(late_sem.at[1 - e], inc=1, device_id={"ta": ta_at[e]},
+                                                        device_id_type=MESH))
     when(has_xl[1], lambda: send_rims(1))
     when(has_xl[0], lambda: start_all(rims[0]))
-    for p in range(EARLY, n_pairs):
+    load_samples(x_left, 0, every_row, 0).wait()
+    for p in range(n_pairs):
         bin_pair(p, x_left, slice(0, LANES))
     pack_halo(1)
     when(has_ta[1], lambda: start_all(halos[1]))
+    late(1)
     load_samples(x_right, LANES, every_row, 1).wait()
-    for p in range(n_pairs // 2):
+    for p in range(n_pairs):
         bin_pair(p, x_right, slice(LANES, span))
 
-    def late():
-        pl.semaphore_wait(late_sem, 2 * count_ta)
-        when(has_xl[0], lambda: send_diags(0))
-
     first = (xl == 0) & (ta == 0)
-    when(jnp.logical_not(first), late)
-    for p in range(n_pairs // 2, n_pairs):
-        bin_pair(p, x_right, slice(LANES, span))
+    when(jnp.logical_not(first), lambda: late(0))
+    for p, r in ends:
+        chosen = [hot[p, r * height: (r + 1) * height] for hot, (_, _, _, height) in zip(hots, ranges)]
+        merge(p, r, [dot(part, jnp.ones((part.shape[1], LANES), BF16)) for part in chosen], slice(span, span + LANES))
+    to_other.start()
     pack_halo(0)
     when(has_ta[0], lambda: start_all(halos[0]))
     for p in range(n_pairs):
         count_pair(p)
-    to_other.start()
-    when(first, late)
+    when(first, lambda: late(0))
 
     def resample(values):
         high, low = halves(values)
@@ -268,10 +290,7 @@
             acc[b + 1] = acc[b + 1] + il_recv[...]
         main[b] = resample(acc[b + 1, :, :span])
     for d in range(2):
-        def arrived(d=d):
-            for copy in rims[d]:
-                copy.wait_recv()
-        when(has_xl[1 - d], arrived)
+        when(has_xl[1 - d], lambda d=d: wait_rims(recv_sem, d))
     sub = lax.broadcasted_iota(jnp.int32, (n_pairs, 1), 0)
     rim = jnp.concatenate([rim_recv[d] + jnp.where(sub == own_row, corner_recv[d], 0.0) for d in range(2)], axis=0)
     more = resample(rim[:, :span])
@@ -291,36 +310,20 @@
 
     for d in range(2):
         for e in range(2):
-            def diag_arrived(d=d, e=e):
-                for copy in diags[d, e]:
-                    copy.wait_recv()
-            when(has_xl[1 - d] & has_ta[1 - e], diag_arrived)
+            when(has_xl[1 - d] & has_ta[1 - e], lambda d=d, e=e: wait_diags(recv_sem, d, e))
     for d in range(2):
         first, last = [diag_recv[d, e] + jnp.where(sub == own_row, diag_corner[d, e], 0.0) for e in (1, 0)]
         rim_out[d * n_pairs: (d + 1) * n_pairs] = jnp.where(is_first, first, jnp.where(is_last, last, 0.0))
     for e in range(2):
-        def halo_arrived(e=e):
-            for copy in halos[e]:
-                copy.wait_recv()
-        when(has_ta[1 - e], halo_arrived)
-        halo_out[e] = halo_recv[e]
-        halo_out[e, own_row] = halo_recv[e, own_row] + halo_rim_recv[e]
+        when(has_ta[1 - e], lambda e=e: wait_halos(recv_sem, e))
+        halo_out[e] = halo_recv[e, :n_pairs]
+        halo_out[e, own_row] = halo_recv[e, own_row] + halo_recv[e, n_pairs]
     to_other.wait_send()
     for d in range(2):
-        def sent(d=d):
-            for copy in rims[d]:
-                copy.wait_send()
-            for e in range(2):
-                def diag_sent(d=d, e=e):
-                    for copy in diags[d, e]:
-                        copy.wait_send()
-                when(has_ta[e], diag_sent)
-        when(has_xl[d], sent)
-
-        def halo_sent(d=d):
-            for copy in halos[d]:
-                copy.wait_send()
-        when(has_ta[d], halo_sent)
+        when(has_xl[d], lambda d=d: wait_rims(send_sem, d))
+        when(has_ta[d], lambda d=d: wait_halos(send_sem, d))
+        for e in range(2):
+            when(has_xl[d] & has_ta[e], lambda d=d, e=e: wait_diags(send_sem, d, e))
 
 
 def finish(main, factor, halo, rim, t_edge, t_rim, out, staged, out_sem):
@@ -389,16 +392,15 @@
             pltpu.VMEM((2, n_pairs, width), F32),
             pltpu.VMEM((2, 1, width), F32),
             pltpu.VMEM((own_cols, width), F32),
-            pltpu.VMEM((2, n_pairs, REACH, LANES), F32),
-            pltpu.VMEM((2, REACH, LANES), F32),
-            pltpu.VMEM((2, n_pairs, REACH, LANES), F32),
-            pltpu.VMEM((2, REACH, LANES), F32),
+            pltpu.VMEM((2, n_pairs + 1, REACH, LANES), F32),
+            pltpu.VMEM((2, n_pairs + 1, REACH, LANES), F32),
+            pltpu.VMEM((n_pairs + 1, 1, width), F32),
             pltpu.VMEM((2, 2, n_pairs, LANES), F32),
             pltpu.VMEM((2, 2, 1, LANES), F32),
             pltpu.SemaphoreType.DMA((6,)),
-            pltpu.SemaphoreType.REGULAR,
-            pltpu.SemaphoreType.DMA((17,)),
-            pltpu.SemaphoreType.DMA((17,)),
+            pltpu.SemaphoreType.REGULAR((2,)),
+            pltpu.SemaphoreType.DMA((9,)),
+            pltpu.SemaphoreType.DMA((9,)),
         ],
         compiler_params=pltpu.CompilerParams(collective_id=0, has_side_effects=True, vmem_limit_bytes=24 * 2**20),
         name="binning",

time: 9.6 us -> 8.87 us (0.924)
  the two profiles are of different devices: /device:TPU:5 before, /device:TPU:0 now
where the time goes in v3:
time: 8.87 us; the launch traced here: 8.73 us
  Pallas kernels  8.7 us (98%)
    pallas_call x1, Pallas kernels, shards(): pl.pallas_call(functools.partial(binning, n_xl, n_ta), out_shape=(pltpu.V...  7.57 us
    pallas_call x1, Pallas kernels, shards(): pl.pallas_call(finish, out_shape=jax.ShapeDtypeStruct((n_pairs, own_cols,...  1.13 us

profile of v3, /device:TPU:0, one launch (start us, length us, event | category | flops | bytes accessed | tf_op | source)
XLA Modules:
  0.0 8.7 jit_solution(15383021425834144921)
XLA Ops:
  0.0 0.0 copy-start
  0.0 0.0 copy-start.1
  0.0 7.6 %binning.1 = (f32[8,104,384]{2,1,0:T(8,128)S(1)}, f32[8,104,128]{2,1,0:T(8,128)S(1)}, f32[2,8,8,128]{3,2,1,0:T(8,128)S(1)}, f32[16,128]{1,0:T(8,128)S(1)}) custom-call(f32[16,208,256]{2,1,0:T(8,128)} %traces.1, s32[2,16,208]{2,1,0:T(8,128)} %steps_hbm.1, bf16[2,256,384]{2,1,0:T(8,128)(2,1)} %constant.6.clone.tables_hbm), custom_call_target="tpu_custom_call" | custom-call | tf_op jit(solution)/shard_map/binning/pallas_call | solution.py:374
  7.6 0.0 copy-done
  7.6 0.0 copy-done.1
  7.6 1.1 %finish.1 = f32[8,104,384]{2,1,0:T(8,128)} custom-call(f32[8,104,384]{2,1,0:T(8,128)S(1)} %get-tuple-element.9.main, f32[8,104,128]{2,1,0:T(8,128)S(1)} %get-tuple-element.10.factor, f32[2,8,8,128]{3,2,1,0:T(8,128)S(1)} %get-tuple-element.11.halo, f32[16,128]{1,0:T(8,128)S(1)} %get-tuple-element.12.rim, bf16[48,256]{1,0:T(8,128)(2,1)S(1)} %copy-done.1, ...), custom_call_target="tpu_custom_call" | custom-call | tf_op jit(solution)/shard_map/finish/pallas_call | solution.py:408
Async XLA Ops:
  0.0 7.6 %copy-start = (bf16[384,256]{1,0:T(8,128)(2,1)S(1)}, bf16[384,256]{1,0:T(8,128)(2,1)}, u32[]{:S(2)}) copy-start(bf16[384,256]{1,0:T(8,128)(2,1)} %constant.8.clone.t_rim) | copy-start | bytes 589828
  0.0 7.6 %copy-start.1 = (bf16[48,256]{1,0:T(8,128)(2,1)S(1)}, bf16[48,256]{1,0:T(8,128)(2,1)}, u32[]{:S(2)}) copy-start(bf16[48,256]{1,0:T(8,128)(2,1)} %constant.7.clone.t_edge) | copy-start | bytes 73732

commit v4 on v3

--- a/solution.py
+++ b/solution.py
@@ -50,10 +50,16 @@
     return (0, LANES, 0, height), (LANES, n_cols, first, own_cols - first)
 
 
+def scoped(kernel, *semaphores):
+    def run(*refs):
+        pl.run_scoped(lambda *scratch: kernel(*refs, *scratch), *semaphores)
+    return run
+
+
 def binning(n_xl, n_ta, traces, steps_hbm, tables_hbm, main, factor, halo_out, rim_out,
             x_left, x_right, edge_x, steps, tables, keys, hot_a, hot_b, acc,
             rim_send, corner_send, rim_recv, corner_recv, il_recv, halo_send, halo_recv, wide_rows,
-            diag_recv, diag_corner, load_sem, late_sem, send_sem, recv_sem):
+            diag_recv, diag_corner, load_sem, late_sem, recv_sem):
     n_rows, n_cols, _ = x_left.shape
     span = LANES + x_right.shape[2]
     n_pairs, own_cols = n_rows // 2, n_cols // 2
@@ -133,6 +139,13 @@
         rows = lax.broadcasted_iota(jnp.int32, (height, key.shape[1]), 0)
         return jnp.where(rows == key, 1.0, 0.0).astype(BF16)
 
+    for p in range(n_pairs):
+        key = jnp.concatenate([keys[0, 2 * p: 2 * p + 1], keys[0, 2 * p + 1: 2 * p + 2]], axis=1)
+        hot_a[p] = one_hot(key, 3 * ranges[0][3])
+        second = keys[2, 2 * p + 1: 2 * p + 2]
+        key = jnp.concatenate([jnp.where(lane < rest, keys[1, 2 * p: 2 * p + 1], second),
+                               second[:, :2 * rest - LANES]], axis=1)
+        hot_b[p] = one_hot(key, 3 * ranges[1][3])
     rim_bin = bin_row - 1 + lax.shift_right_logical(row, 1)
     outside = jnp.where(il == 0, n_pairs, -1)
     rim_code = jnp.where(rim_bin == outside, n_pairs, jnp.where((rim_bin < 0) | (rim_bin >= n_pairs), -1, rim_bin))
@@ -151,13 +164,6 @@
         corner_send[d, :, :span] = sums[n_pairs: n_pairs + 1]
         corner_send[d, :, span:] = ends[n_pairs: n_pairs + 1]
 
-    for p in range(n_pairs):
-        key = jnp.concatenate([keys[0, 2 * p: 2 * p + 1], keys[0, 2 * p + 1: 2 * p + 2]], axis=1)
-        hot_a[p] = one_hot(key, 3 * ranges[0][3])
-        second = keys[2, 2 * p + 1: 2 * p + 2]
-        key = jnp.concatenate([jnp.where(lane < rest, keys[1, 2 * p: 2 * p + 1], second),
-                               second[:, :2 * rest - LANES]], axis=1)
-        hot_b[p] = one_hot(key, 3 * ranges[1][3])
     hots = (hot_a, hot_b)
     for p in range(n_pairs):
         load_samples(x_right, LANES, pl.ds(2 * p, 2), 1).start()
@@ -191,9 +197,12 @@
             if (p, r) not in ends:
                 merge(p, r, groups(parts, r), slice(span, span + LANES))
 
+    def send_sem(slot):
+        return load_sem.at[(6, 7, 3, 8, 0, 1, 9, 4, 5)[slot]]
+
     def remote(src, dst, slot, partner):
-        return pltpu.make_async_remote_copy(src_ref=src, dst_ref=dst, send_sem=send_sem.at[slot],
-                                            recv_sem=recv_sem.at[slot], device_id=partner, device_id_type=MESH)
+        return pltpu.make_async_remote_copy(src_ref=src, dst_ref=dst, send_sem=send_sem(slot), recv_sem=recv_sem.at[slot],
+                                            device_id=partner, device_id_type=MESH)
 
     rim_row = jnp.where(il == 0, n_pairs + 1, 0)
     own_row = jnp.where(il == 0, n_pairs - 1, 0)
@@ -212,8 +221,11 @@
             diags[d, e] = (remote(rim_send.at[d, :, end], diag_recv.at[d, e], slot, to),
                            remote(corner_send.at[d, :, end], diag_corner.at[d, e], slot, {"il": other, **to}))
 
+    def received(slot):
+        return recv_sem.at[slot]
+
     def wait_all(semaphores, slot, rows):
-        pltpu.make_async_copy(rows, rows, semaphores.at[slot]).wait()
+        pltpu.make_async_copy(rows, rows, semaphores(slot)).wait()
 
     def wait_rims(semaphores, d):
         wait_all(semaphores, 1 + d, wide_rows)
@@ -290,7 +302,7 @@
             acc[b + 1] = acc[b + 1] + il_recv[...]
         main[b] = resample(acc[b + 1, :, :span])
     for d in range(2):
-        when(has_xl[1 - d], lambda d=d: wait_rims(recv_sem, d))
+        when(has_xl[1 - d], lambda d=d: wait_rims(received, d))
     sub = lax.broadcasted_iota(jnp.int32, (n_pairs, 1), 0)
     rim = jnp.concatenate([rim_recv[d] + jnp.where(sub == own_row, corner_recv[d], 0.0) for d in range(2)], axis=0)
     more = resample(rim[:, :span])
@@ -310,12 +322,12 @@
 
     for d in range(2):
         for e in range(2):
-            when(has_xl[1 - d] & has_ta[1 - e], lambda d=d, e=e: wait_diags(recv_sem, d, e))
+            when(has_xl[1 - d] & has_ta[1 - e], lambda d=d, e=e: wait_diags(received, d, e))
     for d in range(2):
         first, last = [diag_recv[d, e] + jnp.where(sub == own_row, diag_corner[d, e], 0.0) for e in (1, 0)]
         rim_out[d * n_pairs: (d + 1) * n_pairs] = jnp.where(is_first, first, jnp.where(is_last, last, 0.0))
     for e in range(2):
-        when(has_ta[1 - e], lambda e=e: wait_halos(recv_sem, e))
+        when(has_ta[1 - e], lambda e=e: wait_halos(received, e))
         halo_out[e] = halo_recv[e, :n_pairs]
         halo_out[e, own_row] = halo_recv[e, own_row] + halo_recv[e, n_pairs]
     to_other.wait_send()
@@ -372,7 +384,8 @@
     hbm = pl.BlockSpec(memory_space=pltpu.HBM)
     (start_a, stop_a, _, height_a), (start_b, stop_b, _, height_b) = column_ranges(n_cols)
     main, factor, halo, rim = pl.pallas_call(
-        functools.partial(binning, n_xl, n_ta),
+        scoped(functools.partial(binning, n_xl, n_ta), pltpu.SemaphoreType.DMA((10,)), pltpu.SemaphoreType.REGULAR((2,)),
+               pltpu.SemaphoreType.DMA((9,))),
         out_shape=(pltpu.VMEM((n_pairs, own_cols, out_span), F32), pltpu.VMEM((n_pairs, own_cols, LANES), F32),
                    pltpu.VMEM((2, n_pairs, REACH, LANES), F32), pltpu.VMEM((2 * n_pairs, LANES), F32)),
         in_specs=[hbm] * 3,
@@ -397,20 +410,16 @@
             pltpu.VMEM((n_pairs + 1, 1, width), F32),
             pltpu.VMEM((2, 2, n_pairs, LANES), F32),
             pltpu.VMEM((2, 2, 1, LANES), F32),
-            pltpu.SemaphoreType.DMA((6,)),
-            pltpu.SemaphoreType.REGULAR((2,)),
-            pltpu.SemaphoreType.DMA((9,)),
-            pltpu.SemaphoreType.DMA((9,)),
         ],
         compiler_params=pltpu.CompilerParams(collective_id=0, has_side_effects=True, vmem_limit_bytes=24 * 2**20),
         name="binning",
     )(*[pltpu.with_memory_space_constraint(a, pltpu.HBM) for a in (traces, bin_steps, jnp.asarray(tables))])
     return pl.pallas_call(
-        finish,
+        scoped(finish, pltpu.SemaphoreType.DMA((2,))),
         out_shape=jax.ShapeDtypeStruct((n_pairs, own_cols, out_span), F32),
         in_specs=[vmem] * 6,
         out_specs=hbm,
-        scratch_shapes=[pltpu.VMEM((n_pairs, 2, own_cols, LANES), F32), pltpu.SemaphoreType.DMA((2,))],
+        scratch_shapes=[pltpu.VMEM((n_pairs, 2, own_cols, LANES), F32)],
         compiler_params=pltpu.CompilerParams(vmem_limit_bytes=16 * 2**20),
         name="finish",
     )(main, factor, halo, rim, jnp.asarray(t_edge), jnp.asarray(t_rim))

time: 8.87 us -> 8.57 us (0.966)
  Pallas kernels: 8.7 us -> 8.41 us
    pallas_call x2, Pallas kernels: 8.7 us -> 8.41 us  [the longest x1 7.3 us: shards(): pl.pallas_call(scoped(functools.partial(binning, n_xl, n_ta), pltpu.Semap...]
where the time goes in v4:
time: 8.57 us; the launch traced here: 8.43 us
  Pallas kernels  8.41 us (98%)
    pallas_call x1, Pallas kernels, shards(): pl.pallas_call(scoped(functools.partial(binning, n_xl, n_ta), pltpu.Semap...  7.3 us
    pallas_call x1, Pallas kernels, shards(): pl.pallas_call(scoped(finish, pltpu.SemaphoreType.DMA((2,))), out_shape=j...  1.12 us

profile of v4, /device:TPU:0, one launch (start us, length us, event | category | flops | bytes accessed | tf_op | source)
XLA Modules:
  0.0 8.4 jit_solution(15576708438665599464)
XLA Ops:
  0.0 0.0 copy-start
  0.0 0.0 copy-start.1
  0.0 7.3 %binning.1 = (f32[8,104,384]{2,1,0:T(8,128)S(1)}, f32[8,104,128]{2,1,0:T(8,128)S(1)}, f32[2,8,8,128]{3,2,1,0:T(8,128)S(1)}, f32[16,128]{1,0:T(8,128)S(1)}) custom-call(f32[16,208,256]{2,1,0:T(8,128)} %refs_0_.1, s32[2,16,208]{2,1,0:T(8,128)} %refs_1_.1, bf16[2,256,384]{2,1,0:T(8,128)(2,1)} %constant.6.clone.refs_2_), custom_call_target="tpu_custom_call" | custom-call | tf_op jit(solution)/shard_map/binning/pallas_call | solution.py:386
  7.3 0.0 copy-done
  7.3 0.0 copy-done.1
  7.3 1.1 %finish.1 = f32[8,104,384]{2,1,0:T(8,128)} custom-call(f32[8,104,384]{2,1,0:T(8,128)S(1)} %get-tuple-element.9.refs_0_, f32[8,104,128]{2,1,0:T(8,128)S(1)} %get-tuple-element.10.refs_1_, f32[2,8,8,128]{3,2,1,0:T(8,128)S(1)} %get-tuple-element.11.refs_2_, f32[16,128]{1,0:T(8,128)S(1)} %get-tuple-element.12.refs_3_, bf16[48,256]{1,0:T(8,128)(2,1)S(1)} %copy-done.1, ...), custom_call_target="tpu_custom_call" | custom-call | tf_op jit(solution)/shard_map/finish/pallas_call | solution.py:417
Async XLA Ops:
  0.0 7.3 %copy-start = (bf16[384,256]{1,0:T(8,128)(2,1)S(1)}, bf16[384,256]{1,0:T(8,128)(2,1)}, u32[]{:S(2)}) copy-start(bf16[384,256]{1,0:T(8,128)(2,1)} %constant.8.clone.refs_5_) | copy-start | bytes 589828
  0.0 7.3 %copy-start.1 = (bf16[48,256]{1,0:T(8,128)(2,1)S(1)}, bf16[48,256]{1,0:T(8,128)(2,1)}, u32[]{:S(2)}) copy-start(bf16[48,256]{1,0:T(8,128)(2,1)} %constant.7.clone.refs_4_) | copy-start | bytes 73732

commit v5 on v4

--- a/solution.py
+++ b/solution.py
@@ -93,12 +93,13 @@
             pl.semaphore_signal(barrier, inc=1, device_id={"il": other, **partner}, device_id_type=MESH)
         when(has, signal)
 
+    for d in (1, 0):
+        greet(has_xl[d], {"xl": xl_at[d]})
+    for d in (1, 0):
+        greet(has_xl[0] & has_ta[d], {"xl": xl + 1, "ta": ta_at[d]})
+    for d in (1, 0):
+        greet(has_ta[d], {"ta": ta_at[d]})
     pl.semaphore_signal(barrier, inc=1, device_id={"il": other}, device_id_type=MESH)
-    for d in range(2):
-        greet(has_xl[0] & has_ta[d], {"xl": xl + 1, "ta": ta_at[d]})
-    for d in range(2):
-        greet(has_xl[d], {"xl": xl_at[d]})
-        greet(has_ta[d], {"ta": ta_at[d]})
     count_xl, count_ta = [sum(jnp.where(has, 1, 0) for has in pair) for pair in (has_xl, has_ta)]
     peers = 1 + 2 * (count_xl + count_ta + jnp.where(has_xl[1], count_ta, 0))
     for p in range(n_pairs):
@@ -272,9 +273,10 @@
     for p in range(n_pairs):
         bin_pair(p, x_left, slice(0, LANES))
     pack_halo(1)
-    when(has_ta[1], lambda: start_all(halos[1]))
+    when(has_ta[1] & (il == 0), lambda: start_all(halos[1]))
     late(1)
     load_samples(x_right, LANES, every_row, 1).wait()
+    when(has_ta[1] & (il == 1), lambda: start_all(halos[1]))
     for p in range(n_pairs):
         bin_pair(p, x_right, slice(LANES, span))
 
@@ -340,29 +342,44 @@
 
 def finish(main, factor, halo, rim, t_edge, t_rim, out, staged, out_sem):
     n_pairs, own_cols, width = main.shape
-    inner = pl.ds(LANES, width - 2 * LANES)
-    writes = [pltpu.make_async_copy(main.at[:, :, inner], out.at[:, :, inner], out_sem.at[0])]
-    writes[0].start()
-    high = rim[...].astype(BF16)
-    low = (rim[...] - high.astype(F32)).astype(BF16)
-    more = dot(jnp.concatenate([high, low, high], axis=1), t_rim[...])
+    starts = (0, width - LANES)
+    has_before = lax.axis_index("ta") > 0
+
+    def write_tiles(source, start, size, slot):
+        return pltpu.make_async_copy(source, out.at[:, :, pl.ds(start, size)], out_sem.at[slot])
+
+    def from_main(start, size, slot):
+        return write_tiles(main.at[:, :, pl.ds(start, size)], start, size, slot)
+
+    from_main(LANES, width - 2 * LANES, 2).start()
+    pl.when(jnp.logical_not(has_before))(from_main(0, LANES, 0).start)
     ends_row = lax.broadcasted_iota(jnp.int32, (8, 1), 0)
     tops = ((0, 0, 0), (own_cols - 8, 7, n_pairs))
-    for b in range(n_pairs):
-        edges = jnp.concatenate([halo[0, b], halo[1, b]], axis=0)
-        high = edges.astype(BF16).astype(F32)
-        terms = jnp.concatenate([high, edges - high, high], axis=0).T[:own_cols].astype(BF16)
-        ends = dot(terms, t_edge[...])
-        top, bottom = [ends[at: at + 8] + jnp.where(ends_row == where, more[base + b: base + b + 1], 0.0)
-                       for at, where, base in tops]
-        ends = jnp.concatenate([top, ends[8: own_cols - 8], bottom], axis=0)
-        for d, start in enumerate((0, width - LANES)):
-            staged[b, d] = main[b, :, start: start + LANES] + ends[:, d * LANES: (d + 1) * LANES] * factor[b]
-            write = pltpu.make_async_copy(staged.at[b, d], out.at[b, :, pl.ds(start, LANES)], out_sem.at[1])
-            write.start()
-    writes[0].wait()
-    for d, start in enumerate((0, width - LANES)):
-        pltpu.make_async_copy(staged.at[:, d], out.at[:, :, pl.ds(start, LANES)], out_sem.at[1]).wait()
+
+    def add_halo(tiles, table):
+        high = rim[...].astype(BF16)
+        low = (rim[...] - high.astype(F32)).astype(BF16)
+        more = dot(jnp.concatenate([high, low, high], axis=1), t_rim[...])
+        for pair in zip(tiles[::2], tiles[1::2]):
+            terms = []
+            for d, b in pair:
+                high = halo[d, b].astype(BF16).astype(F32)
+                terms += [high, halo[d, b] - high, high]
+            both = dot(jnp.concatenate(terms, axis=0).T[:own_cols].astype(BF16), t_edge[table])
+            for i, (d, b) in enumerate(pair):
+                ends, lanes = both[:, i * LANES: (i + 1) * LANES], slice(d * LANES, (d + 1) * LANES)
+                top, bottom = [ends[at: at + 8] + jnp.where(ends_row == where, more[base + b: base + b + 1, lanes], 0.0)
+                               for at, where, base in tops]
+                ends = jnp.concatenate([top, ends[8: own_cols - 8], bottom], axis=0)
+                staged[d, b] = main[b, :, starts[d]: starts[d] + LANES] + ends * factor[b]
+                pltpu.make_async_copy(staged.at[d, b], out.at[b, :, pl.ds(starts[d], LANES)], out_sem.at[d]).start()
+
+    rows = range(n_pairs)
+    pl.when(has_before)(lambda: add_halo([(d, b) for b in rows for d in range(2)], 0))
+    pl.when(jnp.logical_not(has_before))(lambda: add_halo([(1, b) for b in rows], 1))
+    from_main(LANES, width - 2 * LANES, 2).wait()
+    for d in range(2):
+        write_tiles(staged.at[d], starts[d], LANES, d).wait()
 
 
 def shards(n_xl, n_ta, traces, bin_steps):
@@ -375,8 +392,10 @@
     table = lanczos_table(span)
     tables = np.stack(split_table(table[REACH:-REACH]))
     edge_cols = np.concatenate([table[:, :LANES], table[:, -LANES:]], axis=1)
-    edge_high, edge_low = split_table(np.concatenate([edge_cols[:REACH], edge_cols[-REACH:]]))
-    t_edge = np.concatenate([edge_high, edge_high, edge_low])
+    edge_high, edge_low = split_table(np.stack([edge_cols[:REACH, :LANES], edge_cols[-REACH:, LANES:]]))
+    before, after = np.concatenate([edge_high, edge_high, edge_low], axis=1)
+    none = np.zeros_like(before)
+    t_edge = np.stack([np.block([[first, none], [none, after]]) for first in (before, after)])
     rim_high, rim_low = split_table(np.concatenate(
         [edge_cols[-REACH:], np.zeros((LANES - 2 * REACH, 2 * LANES), np.float32), edge_cols[:REACH]]))
     t_rim = np.concatenate([rim_high, rim_high, rim_low])
@@ -415,11 +434,11 @@
         name="binning",
     )(*[pltpu.with_memory_space_constraint(a, pltpu.HBM) for a in (traces, bin_steps, jnp.asarray(tables))])
     return pl.pallas_call(
-        scoped(finish, pltpu.SemaphoreType.DMA((2,))),
+        scoped(finish, pltpu.SemaphoreType.DMA((3,))),
         out_shape=jax.ShapeDtypeStruct((n_pairs, own_cols, out_span), F32),
         in_specs=[vmem] * 6,
         out_specs=hbm,
-        scratch_shapes=[pltpu.VMEM((n_pairs, 2, own_cols, LANES), F32)],
+        scratch_shapes=[pltpu.VMEM((2, n_pairs, own_cols, LANES), F32)],
         compiler_params=pltpu.CompilerParams(vmem_limit_bytes=16 * 2**20),
         name="finish",
     )(main, factor, halo, rim, jnp.asarray(t_edge), jnp.asarray(t_rim))

time: 8.57 us -> 8.49 us (level)
    pallas_call x1, Pallas kernels: 1.12 us -> 1.03 us  [shards(): pl.pallas_call(scoped(finish, pltpu.SemaphoreType.DMA((3,))), out_shape=j...]
where the time goes in v5:
time: 8.49 us; the launch traced here: 8.35 us
  Pallas kernels  8.33 us (98%)
    pallas_call x1, Pallas kernels, shards(): pl.pallas_call(scoped(functools.partial(binning, n_xl, n_ta), pltpu.Semap...  7.3 us
    pallas_call x1, Pallas kernels, shards(): pl.pallas_call(scoped(finish, pltpu.SemaphoreType.DMA((3,))), out_shape=j...  1.03 us

profile of v5, /device:TPU:0, one launch (start us, length us, event | category | flops | bytes accessed | tf_op | source)
XLA Modules:
  0.0 8.3 jit_solution(6189080879575919052)
XLA Ops:
  0.0 0.0 copy-start
  0.0 0.0 copy-start.1
  0.0 7.3 %binning.1 = (f32[8,104,384]{2,1,0:T(8,128)S(1)}, f32[8,104,128]{2,1,0:T(8,128)S(1)}, f32[2,8,8,128]{3,2,1,0:T(8,128)S(1)}, f32[16,128]{1,0:T(8,128)S(1)}) custom-call(f32[16,208,256]{2,1,0:T(8,128)} %refs_0_.1, s32[2,16,208]{2,1,0:T(8,128)} %refs_1_.1, bf16[2,256,384]{2,1,0:T(8,128)(2,1)} %constant.6.clone.refs_2_), custom_call_target="tpu_custom_call" | custom-call | tf_op jit(solution)/shard_map/binning/pallas_call | solution.py:405
  7.3 0.0 copy-done
  7.3 0.0 copy-done.1
  7.3 1.0 %finish.1 = f32[8,104,384]{2,1,0:T(8,128)} custom-call(f32[8,104,384]{2,1,0:T(8,128)S(1)} %get-tuple-element.9.refs_0_, f32[8,104,128]{2,1,0:T(8,128)S(1)} %get-tuple-element.10.refs_1_, f32[2,8,8,128]{3,2,1,0:T(8,128)S(1)} %get-tuple-element.11.refs_2_, f32[16,128]{1,0:T(8,128)S(1)} %get-tuple-element.12.refs_3_, bf16[2,48,256]{2,1,0:T(8,128)(2,1)S(1)} %copy-done.1, ...), custom_call_target="tpu_custom_call" | custom-call | tf_op jit(solution)/shard_map/finish/pallas_call | solution.py:436
Async XLA Ops:
  0.0 7.3 %copy-start = (bf16[384,256]{1,0:T(8,128)(2,1)S(1)}, bf16[384,256]{1,0:T(8,128)(2,1)}, u32[]{:S(2)}) copy-start(bf16[384,256]{1,0:T(8,128)(2,1)} %constant.8.clone.refs_5_) | copy-start | bytes 589828
  0.0 7.3 %copy-start.1 = (bf16[2,48,256]{2,1,0:T(8,128)(2,1)S(1)}, bf16[2,48,256]{2,1,0:T(8,128)(2,1)}, u32[]{:S(2)}) copy-start(bf16[2,48,256]{2,1,0:T(8,128)(2,1)} %constant.7.clone.refs_4_) | copy-start | bytes 147460

commit v6 on v5

--- a/solution.py
+++ b/solution.py
@@ -13,6 +13,7 @@
 Q = 2
 REACH = TAPS // 2
 LANES = 128
+LOADS = 4
 MESH = pl.DeviceIdType.MESH
 F32, BF16 = jnp.float32, jnp.bfloat16
 
@@ -102,8 +103,9 @@
     pl.semaphore_signal(barrier, inc=1, device_id={"il": other}, device_id_type=MESH)
     count_xl, count_ta = [sum(jnp.where(has, 1, 0) for has in pair) for pair in (has_xl, has_ta)]
     peers = 1 + 2 * (count_xl + count_ta + jnp.where(has_xl[1], count_ta, 0))
-    for p in range(n_pairs):
-        load_samples(x_left, 0, pl.ds(2 * p, 2), 0).start()
+    quarter = n_rows // LOADS
+    for p in range(LOADS):
+        load_samples(x_left, 0, pl.ds(quarter * p, quarter), 0).start()
 
     for e in range(2):
         def no_ta(e=e):
@@ -166,8 +168,8 @@
         corner_send[d, :, span:] = ends[n_pairs: n_pairs + 1]
 
     hots = (hot_a, hot_b)
-    for p in range(n_pairs):
-        load_samples(x_right, LANES, pl.ds(2 * p, 2), 1).start()
+    for p in range(LOADS):
+        load_samples(x_right, LANES, pl.ds(quarter * p, quarter), 1).start()
     table_load.start()
 
     def merge(p, r, parts, lanes):
@@ -264,10 +266,10 @@
 
     every_row = pl.ds(0, n_rows)
     pl.semaphore_wait(barrier, peers)
+    when(has_xl[1], lambda: send_rims(1))
     for e in range(2):
         when(has_ta[e], lambda e=e: pl.semaphore_signal(late_sem.at[1 - e], inc=1, device_id={"ta": ta_at[e]},
                                                         device_id_type=MESH))
-    when(has_xl[1], lambda: send_rims(1))
     when(has_xl[0], lambda: start_all(rims[0]))
     load_samples(x_left, 0, every_row, 0).wait()
     for p in range(n_pairs):
@@ -322,6 +324,13 @@
         factor[b] = scale
         main[b] = add_rows(main[b], more, b) * jnp.concatenate([scale] * (main.shape[2] // LANES), axis=1)
 
+    to_other.wait_send()
+    for d in range(2):
+        when(has_xl[d], lambda d=d: wait_rims(send_sem, d))
+        when(has_ta[d], lambda d=d: wait_halos(send_sem, d))
+        for e in range(2):
+            when(has_xl[d] & has_ta[e], lambda d=d, e=e: wait_diags(send_sem, d, e))
+
     for d in range(2):
         for e in range(2):
             when(has_xl[1 - d] & has_ta[1 - e], lambda d=d, e=e: wait_diags(received, d, e))
@@ -332,12 +341,6 @@
         when(has_ta[1 - e], lambda e=e: wait_halos(received, e))
         halo_out[e] = halo_recv[e, :n_pairs]
         halo_out[e, own_row] = halo_recv[e, own_row] + halo_recv[e, n_pairs]
-    to_other.wait_send()
-    for d in range(2):
-        when(has_xl[d], lambda d=d: wait_rims(send_sem, d))
-        when(has_ta[d], lambda d=d: wait_halos(send_sem, d))
-        for e in range(2):
-            when(has_xl[d] & has_ta[e], lambda d=d, e=e: wait_diags(send_sem, d, e))
 
 
 def finish(main, factor, halo, rim, t_edge, t_rim, out, staged, out_sem):

time: 8.49 us -> 8.47 us (level)
  no operation moved by 1% of the time
where the time goes in v6:
time: 8.47 us; the launch traced here: 8.32 us
  Pallas kernels  8.31 us (98%)
    pallas_call x1, Pallas kernels, shards(): pl.pallas_call(scoped(functools.partial(binning, n_xl, n_ta), pltpu.Semap...  7.29 us
    pallas_call x1, Pallas kernels, shards(): pl.pallas_call(scoped(finish, pltpu.SemaphoreType.DMA((3,))), out_shape=j...  1.02 us

profile of v6, /device:TPU:0, one launch (start us, length us, event | category | flops | bytes accessed | tf_op | source)
XLA Modules:
  0.0 8.3 jit_solution(4702916971245051825)
XLA Ops:
  0.0 0.0 copy-start
  0.0 0.0 copy-start.1
  0.0 7.3 %binning.1 = (f32[8,104,384]{2,1,0:T(8,128)S(1)}, f32[8,104,128]{2,1,0:T(8,128)S(1)}, f32[2,8,8,128]{3,2,1,0:T(8,128)S(1)}, f32[16,128]{1,0:T(8,128)S(1)}) custom-call(f32[16,208,256]{2,1,0:T(8,128)} %refs_0_.1, s32[2,16,208]{2,1,0:T(8,128)} %refs_1_.1, bf16[2,256,384]{2,1,0:T(8,128)(2,1)} %constant.6.clone.refs_2_), custom_call_target="tpu_custom_call" | custom-call | tf_op jit(solution)/shard_map/binning/pallas_call | solution.py:408
  7.3 0.0 copy-done
  7.3 0.0 copy-done.1
  7.3 1.0 %finish.1 = f32[8,104,384]{2,1,0:T(8,128)} custom-call(f32[8,104,384]{2,1,0:T(8,128)S(1)} %get-tuple-element.9.refs_0_, f32[8,104,128]{2,1,0:T(8,128)S(1)} %get-tuple-element.10.refs_1_, f32[2,8,8,128]{3,2,1,0:T(8,128)S(1)} %get-tuple-element.11.refs_2_, f32[16,128]{1,0:T(8,128)S(1)} %get-tuple-element.12.refs_3_, bf16[2,48,256]{2,1,0:T(8,128)(2,1)S(1)} %copy-done.1, ...), custom_call_target="tpu_custom_call" | custom-call | tf_op jit(solution)/shard_map/finish/pallas_call | solution.py:439
Async XLA Ops:
  0.0 7.3 %copy-start = (bf16[384,256]{1,0:T(8,128)(2,1)S(1)}, bf16[384,256]{1,0:T(8,128)(2,1)}, u32[]{:S(2)}) copy-start(bf16[384,256]{1,0:T(8,128)(2,1)} %constant.8.clone.refs_5_) | copy-start | bytes 589828
  0.0 7.3 %copy-start.1 = (bf16[2,48,256]{2,1,0:T(8,128)(2,1)S(1)}, bf16[2,48,256]{2,1,0:T(8,128)(2,1)}, u32[]{:S(2)}) copy-start(bf16[2,48,256]{2,1,0:T(8,128)(2,1)} %constant.7.clone.refs_4_) | copy-start | bytes 147460

commit v7 on v6

--- a/solution.py
+++ b/solution.py
@@ -73,6 +73,18 @@
     def when(condition, work):
         pl.when(condition)(work)
 
+    barrier = pltpu.get_barrier_semaphore()
+
+    def greet(has, partner):
+        def signal():
+            pl.semaphore_signal(barrier, inc=1, device_id=partner, device_id_type=MESH)
+            pl.semaphore_signal(barrier, inc=1, device_id={"il": other, **partner}, device_id_type=MESH)
+        when(has, signal)
+
+    greet(has_ta[1], {"ta": ta - 1})
+    greet(has_xl[1], {"xl": xl - 1})
+    greet(has_xl[0] & has_ta[1], {"xl": xl + 1, "ta": ta - 1})
+
     step_load = pltpu.make_async_copy(steps_hbm, steps, load_sem.at[3])
     step_load.start()
     edge_loads = [pltpu.make_async_copy(traces.at[:, pl.ds(start, 8)], edge_x.at[d], load_sem.at[4 + d])
@@ -86,26 +98,16 @@
 
     table_load = pltpu.make_async_copy(tables_hbm, tables, load_sem.at[2])
 
-    barrier = pltpu.get_barrier_semaphore()
-
-    def greet(has, partner):
-        def signal():
-            pl.semaphore_signal(barrier, inc=1, device_id=partner, device_id_type=MESH)
-            pl.semaphore_signal(barrier, inc=1, device_id={"il": other, **partner}, device_id_type=MESH)
-        when(has, signal)
-
-    for d in (1, 0):
-        greet(has_xl[d], {"xl": xl_at[d]})
-    for d in (1, 0):
-        greet(has_xl[0] & has_ta[d], {"xl": xl + 1, "ta": ta_at[d]})
-    for d in (1, 0):
-        greet(has_ta[d], {"ta": ta_at[d]})
+    quarter = n_rows // LOADS
+    for p in range(LOADS):
+        load_samples(x_left, 0, pl.ds(quarter * p, quarter), 0).start()
+
+    greet(has_xl[0] & has_ta[0], {"xl": xl + 1, "ta": ta + 1})
+    greet(has_xl[0], {"xl": xl + 1})
+    greet(has_ta[0], {"ta": ta + 1})
     pl.semaphore_signal(barrier, inc=1, device_id={"il": other}, device_id_type=MESH)
     count_xl, count_ta = [sum(jnp.where(has, 1, 0) for has in pair) for pair in (has_xl, has_ta)]
     peers = 1 + 2 * (count_xl + count_ta + jnp.where(has_xl[1], count_ta, 0))
-    quarter = n_rows // LOADS
-    for p in range(LOADS):
-        load_samples(x_left, 0, pl.ds(quarter * p, quarter), 0).start()
 
     for e in range(2):
         def no_ta(e=e):
@@ -265,31 +267,37 @@
         when(has_ta[e], go)
 
     every_row = pl.ds(0, n_rows)
+    def bin_left():
+        load_samples(x_left, 0, every_row, 0).wait()
+        for p in range(n_pairs):
+            bin_pair(p, x_left, slice(0, LANES))
+        pack_halo(1)
+
+    first = (xl == 0) & (ta == 0)
+    opens_late = first | (xl >= 2)
+    when(opens_late, bin_left)
     pl.semaphore_wait(barrier, peers)
     when(has_xl[1], lambda: send_rims(1))
     for e in range(2):
         when(has_ta[e], lambda e=e: pl.semaphore_signal(late_sem.at[1 - e], inc=1, device_id={"ta": ta_at[e]},
                                                         device_id_type=MESH))
     when(has_xl[0], lambda: start_all(rims[0]))
-    load_samples(x_left, 0, every_row, 0).wait()
-    for p in range(n_pairs):
-        bin_pair(p, x_left, slice(0, LANES))
-    pack_halo(1)
-    when(has_ta[1] & (il == 0), lambda: start_all(halos[1]))
+    when(jnp.logical_not(opens_late), bin_left)
+    when(has_ta[1], halos[1][1].start)
+    when(has_ta[1], halos[1][0].start)
     late(1)
     load_samples(x_right, LANES, every_row, 1).wait()
-    when(has_ta[1] & (il == 1), lambda: start_all(halos[1]))
     for p in range(n_pairs):
         bin_pair(p, x_right, slice(LANES, span))
 
-    first = (xl == 0) & (ta == 0)
-    when(jnp.logical_not(first), lambda: late(0))
+    when(jnp.logical_not(opens_late), lambda: late(0))
+    pack_halo(0)
+    when(has_ta[0], lambda: start_all(halos[0]))
+    when(xl >= 2, lambda: late(0))
     for p, r in ends:
         chosen = [hot[p, r * height: (r + 1) * height] for hot, (_, _, _, height) in zip(hots, ranges)]
         merge(p, r, [dot(part, jnp.ones((part.shape[1], LANES), BF16)) for part in chosen], slice(span, span + LANES))
     to_other.start()
-    pack_halo(0)
-    when(has_ta[0], lambda: start_all(halos[0]))
     for p in range(n_pairs):
         count_pair(p)
     when(first, lambda: late(0))

time: 8.47 us -> 8.42 us (level)
  no operation moved by 1% of the time
where the time goes in v7:
time: 8.42 us; the launch traced here: 8.27 us
  Pallas kernels  8.26 us (98%)
    pallas_call x1, Pallas kernels, shards(): pl.pallas_call(scoped(functools.partial(binning, n_xl, n_ta), pltpu.Semap...  7.24 us
    pallas_call x1, Pallas kernels, shards(): pl.pallas_call(scoped(finish, pltpu.SemaphoreType.DMA((3,))), out_shape=j...  1.02 us

profile of v7, /device:TPU:0, one launch (start us, length us, event | category | flops | bytes accessed | tf_op | source)
XLA Modules:
  0.0 8.3 jit_solution(10401827976063390608)
XLA Ops:
  0.0 0.0 copy-start
  0.0 0.0 copy-start.1
  0.0 7.2 %binning.1 = (f32[8,104,384]{2,1,0:T(8,128)S(1)}, f32[8,104,128]{2,1,0:T(8,128)S(1)}, f32[2,8,8,128]{3,2,1,0:T(8,128)S(1)}, f32[16,128]{1,0:T(8,128)S(1)}) custom-call(f32[16,208,256]{2,1,0:T(8,128)} %refs_0_.1, s32[2,16,208]{2,1,0:T(8,128)} %refs_1_.1, bf16[2,256,384]{2,1,0:T(8,128)(2,1)} %constant.6.clone.refs_2_), custom_call_target="tpu_custom_call" | custom-call | tf_op jit(solution)/shard_map/binning/pallas_call | solution.py:416
  7.2 0.0 copy-done
  7.2 0.0 copy-done.1
  7.2 1.0 %finish.1 = f32[8,104,384]{2,1,0:T(8,128)} custom-call(f32[8,104,384]{2,1,0:T(8,128)S(1)} %get-tuple-element.9.refs_0_, f32[8,104,128]{2,1,0:T(8,128)S(1)} %get-tuple-element.10.refs_1_, f32[2,8,8,128]{3,2,1,0:T(8,128)S(1)} %get-tuple-element.11.refs_2_, f32[16,128]{1,0:T(8,128)S(1)} %get-tuple-element.12.refs_3_, bf16[2,48,256]{2,1,0:T(8,128)(2,1)S(1)} %copy-done.1, ...), custom_call_target="tpu_custom_call" | custom-call | tf_op jit(solution)/shard_map/finish/pallas_call | solution.py:447
Async XLA Ops:
  0.0 7.2 %copy-start = (bf16[384,256]{1,0:T(8,128)(2,1)S(1)}, bf16[384,256]{1,0:T(8,128)(2,1)}, u32[]{:S(2)}) copy-start(bf16[384,256]{1,0:T(8,128)(2,1)} %constant.8.clone.refs_5_) | copy-start | bytes 589828
  0.0 7.2 %copy-start.1 = (bf16[2,48,256]{2,1,0:T(8,128)(2,1)S(1)}, bf16[2,48,256]{2,1,0:T(8,128)(2,1)}, u32[]{:S(2)}) copy-start(bf16[2,48,256]{2,1,0:T(8,128)(2,1)} %constant.7.clone.refs_4_) | copy-start | bytes 147460

commit v8 on v7

--- a/solution.py
+++ b/solution.py
@@ -283,8 +283,7 @@
                                                         device_id_type=MESH))
     when(has_xl[0], lambda: start_all(rims[0]))
     when(jnp.logical_not(opens_late), bin_left)
-    when(has_ta[1], halos[1][1].start)
-    when(has_ta[1], halos[1][0].start)
+    when(has_ta[1], lambda: start_all(halos[1]))
     late(1)
     load_samples(x_right, LANES, every_row, 1).wait()
     for p in range(n_pairs):

time: 8.42 us -> 8.37 us (level)
  no operation moved by 1% of the time
where the time goes in v8:
time: 8.37 us; the launch traced here: 8.23 us
  Pallas kernels  8.22 us (98%)
    pallas_call x1, Pallas kernels, shards(): pl.pallas_call(scoped(functools.partial(binning, n_xl, n_ta), pltpu.Semap...  7.2 us
    pallas_call x1, Pallas kernels, shards(): pl.pallas_call(scoped(finish, pltpu.SemaphoreType.DMA((3,))), out_shape=j...  1.02 us

profile of v8, /device:TPU:0, one launch (start us, length us, event | category | flops | bytes accessed | tf_op | source)
XLA Modules:
  0.0 8.2 jit_solution(6186828764580272064)
XLA Ops:
  0.0 0.0 copy-start
  0.0 0.0 copy-start.1
  0.0 7.2 %binning.1 = (f32[8,104,384]{2,1,0:T(8,128)S(1)}, f32[8,104,128]{2,1,0:T(8,128)S(1)}, f32[2,8,8,128]{3,2,1,0:T(8,128)S(1)}, f32[16,128]{1,0:T(8,128)S(1)}) custom-call(f32[16,208,256]{2,1,0:T(8,128)} %refs_0_.1, s32[2,16,208]{2,1,0:T(8,128)} %refs_1_.1, bf16[2,256,384]{2,1,0:T(8,128)(2,1)} %constant.6.clone.refs_2_), custom_call_target="tpu_custom_call" | custom-call | tf_op jit(solution)/shard_map/binning/pallas_call | solution.py:415
  7.2 0.0 copy-done
  7.2 0.0 copy-done.1
  7.2 1.0 %finish.1 = f32[8,104,384]{2,1,0:T(8,128)} custom-call(f32[8,104,384]{2,1,0:T(8,128)S(1)} %get-tuple-element.9.refs_0_, f32[8,104,128]{2,1,0:T(8,128)S(1)} %get-tuple-element.10.refs_1_, f32[2,8,8,128]{3,2,1,0:T(8,128)S(1)} %get-tuple-element.11.refs_2_, f32[16,128]{1,0:T(8,128)S(1)} %get-tuple-element.12.refs_3_, bf16[2,48,256]{2,1,0:T(8,128)(2,1)S(1)} %copy-done.1, ...), custom_call_target="tpu_custom_call" | custom-call | tf_op jit(solution)/shard_map/finish/pallas_call | solution.py:446
Async XLA Ops:
  0.0 7.2 %copy-start = (bf16[384,256]{1,0:T(8,128)(2,1)S(1)}, bf16[384,256]{1,0:T(8,128)(2,1)}, u32[]{:S(2)}) copy-start(bf16[384,256]{1,0:T(8,128)(2,1)} %constant.8.clone.refs_5_) | copy-start | bytes 589828
  0.0 7.2 %copy-start.1 = (bf16[2,48,256]{2,1,0:T(8,128)(2,1)S(1)}, bf16[2,48,256]{2,1,0:T(8,128)(2,1)}, u32[]{:S(2)}) copy-start(bf16[2,48,256]{2,1,0:T(8,128)(2,1)} %constant.7.clone.refs_4_) | copy-start | bytes 147460
